TPU v7x, 32 devices: a whole 2x2x4 slice. The times are simulated.
32 devices in a mesh: wide: 8 (over y, x, core), head: 4 (over z).
Axes of the slice: x: 2, y: 2, z: 4, core: 2. Of those that a mesh axis runs over, the one named last changes fastest.
Arguments:
- tokens: bfloat16 [16384, 1024], P(('wide', 'head')), may hold values from -6 to 6
- cotangent: bfloat16 [16384, 1024], P(('wide', 'head')), may hold values from -6 to 6
- w_query: bfloat16 [1024, 1024], P('wide', 'head'), may hold values from -0.25 to 0.25
- w_key: bfloat16 [1024, 1024], P('wide', 'head'), may hold values from -0.25 to 0.25
- w_value: bfloat16 [1024, 1024], P('wide', 'head'), may hold values from -0.1875 to 0.1875
- w_out: bfloat16 [1024, 1024], P('head', 'wide'), may hold values from -0.1875 to 0.1875
- w_up: bfloat16 [1024, 4096], P('wide', 'head'), may hold values from -0.1875 to 0.1875
- w_down: bfloat16 [4096, 1024], P('head', 'wide'), may hold values from -0.09375 to 0.09375
- norm_gain: float32 [4, 1024], replicated, may hold values from 0.25 to 1.75
- norm_bias: float32 [4, 1024], replicated, may hold values from -3 to 3
Outputs:
- block_out: bfloat16 [16384, 1024], P(('wide', 'head'))
- input_grad: float32 [16384, 1024], P(('wide', 'head'))
- grad_query: float32 [1024, 1024], P('wide', 'head')
- grad_key: float32 [1024, 1024], P('wide', 'head')
- grad_value: float32 [1024, 1024], P('wide', 'head')
- grad_out: float32 [1024, 1024], P('head', 'wide')
- grad_up: float32 [1024, 4096], P('wide', 'head')
- grad_down: float32 [4096, 1024], P('head', 'wide')
- gain_grad: float32 [4, 1024], replicated
- bias_grad: float32 [4, 1024], replicated
All inputs are finite; a program needn't handle non-finite values.
Results may differ from a plain program's by a relative error of at most 0.015.
Values may be sent and summed in bfloat16 or wider, within the bound.
No kernel may reach another device: no remote copies, remote signals or barrier semaphores. Data moves between devices by JAX's collectives and lax.ppermute only.
A program may use at most 192 MiB of HBM per device.

v0:
```python
import math

import jax
import jax.numpy as jnp
from jax import lax
from jax.sharding import Mesh, PartitionSpec as P


HD = 64


EPS = 1e-05


def normalize(values, gain, bias):
    average = jnp.mean(values, axis=-1, keepdims=True)
    centred = values - average
    inverse = lax.rsqrt(jnp.mean(centred * centred, axis=-1, keepdims=True) + EPS)
    unit_rows = centred * inverse
    return (unit_rows * gain + bias, unit_rows, inverse)


def normalize_back(gradient, unit_rows, inverse, gain):
    scaled = gradient * gain
    inner_sum = (
        scaled
        - jnp.mean(scaled, axis=-1, keepdims=True)
        - unit_rows * jnp.mean(scaled * unit_rows, axis=-1, keepdims=True)
    )
    return (inner_sum * inverse, jnp.sum(gradient * unit_rows, axis=0), jnp.sum(gradient, axis=0))


def masked_scores(rows_q, key_heads, first_row, score_scale):
    scores = (
        jnp.einsum("qgd,kgd->gqk", rows_q, key_heads, preferred_element_type=jnp.float32)
        * score_scale
    )
    place_q = first_row + jnp.arange(rows_q.shape[0], dtype=jnp.int32)
    place_k = jnp.arange(key_heads.shape[0], dtype=jnp.int32)
    allowed = place_k[None, :] <= place_q[:, None]
    return jnp.where(allowed[None], scores, -1e30)


def attend(queries, key_rows, value_rows, block_rows):
    length, width = queries.shape
    groups = width // HD
    score_scale = 1.0 / math.sqrt(HD)
    query_heads = queries.reshape(length, groups, HD)
    key_heads = key_rows.reshape(length, groups, HD)
    value_heads = value_rows.reshape(length, groups, HD)
    out_blocks = []
    totals = []
    for position in range(length // block_rows):
        first_row = position * block_rows
        last_row = first_row + block_rows
        scores = masked_scores(
            query_heads[first_row:last_row], key_heads[:last_row], first_row, score_scale
        )
        row_max = jnp.max(scores, axis=-1, keepdims=True)
        exp_scores = jnp.exp(scores - row_max)
        row_total = jnp.sum(exp_scores, axis=-1, keepdims=True)
        weights = (exp_scores / row_total).astype(jnp.bfloat16)
        out_blocks.append(
            jnp.einsum(
                "gqk,kgd->qgd", weights, value_heads[:last_row], preferred_element_type=jnp.float32
            )
        )
        totals.append(row_max + jnp.log(row_total))
    return (jnp.concatenate(out_blocks, axis=0).reshape(length, width), totals)


def attend_back(queries, key_rows, value_rows, grad_rows, totals, block_rows, first):
    length, width = queries.shape
    groups = width // HD
    score_scale = 1.0 / math.sqrt(HD)
    query_heads = queries.reshape(length, groups, HD)
    key_heads = key_rows.reshape(length, groups, HD)
    value_heads = value_rows.reshape(length, groups, HD)
    grad_heads = grad_rows.reshape(length, groups, HD)
    grad_keys = jnp.zeros((length, groups, HD), jnp.float32)
    grad_values = jnp.zeros((length, groups, HD), jnp.float32)
    query_parts = []
    for position in range(length // block_rows):
        first_row = position * block_rows
        last_row = first_row + block_rows
        rows_q = query_heads[first_row:last_row]
        if last_row == length:
            rows_q, grad_rows = lax.optimization_barrier(((rows_q, grad_heads), first))[0]
            grad_heads = grad_rows
        scores = masked_scores(rows_q, key_heads[:last_row], first_row, score_scale)
        weights = jnp.exp(scores - totals[position])
        rounded = weights.astype(jnp.bfloat16)
        grad_block = grad_heads[first_row:last_row]
        grad_values = grad_values.at[:last_row].add(
            jnp.einsum("gqk,qgd->kgd", rounded, grad_block, preferred_element_type=jnp.float32)
        )
        grad_weights = jnp.einsum(
            "qgd,kgd->gqk", grad_block, value_heads[:last_row], preferred_element_type=jnp.float32
        )
        inner_sum = jnp.sum(weights * grad_weights, axis=-1, keepdims=True)
        grad_scores = (weights * (grad_weights - inner_sum)).astype(jnp.bfloat16)
        query_parts.append(
            jnp.einsum(
                "gqk,kgd->qgd",
                grad_scores,
                key_heads[:last_row],
                preferred_element_type=jnp.float32,
            )
            * score_scale
        )
        grad_keys = grad_keys.at[:last_row].add(
            jnp.einsum("gqk,qgd->kgd", grad_scores, rows_q, preferred_element_type=jnp.float32)
            * score_scale
        )
    grad_queries = jnp.concatenate(query_parts, axis=0).reshape(length, width).astype(jnp.bfloat16)
    return (
        grad_queries,
        grad_keys.reshape(length, width).astype(jnp.bfloat16),
        grad_values.reshape(length, width).astype(jnp.bfloat16),
    )


def contract_rows(left_op, right_op):
    return lax.dot_general(
        left_op, right_op, (((0,), (0,)), ((), ())), preferred_element_type=jnp.float32
    )


def contract_cols(left_op, right_op):
    return lax.dot_general(
        left_op, right_op, (((1,), (1,)), ((), ())), preferred_element_type=jnp.float32
    )


WIDE = ("outer", "pair")
ALL = ("outer", "pair", "head")
LINE = ("pair", "head")
HEADS = 4


def swap(values):
    return lax.ppermute(values, "pair", [(0, 1), (1, 0)])


def send(values, moves):
    return lax.ppermute(values, LINE, [(a * HEADS + b, c * HEADS + d) for (a, b), (c, d) in moves])


def both(moves):
    return [((p, a), (p, b)) for p in range(2) for a, b in moves]


def shift(values, step):
    return lax.ppermute(values, "head", [(i, (i + step) % HEADS) for i in range(HEADS)])


def halves(block, axis):
    size = block.shape[axis] // 2
    place = lax.axis_index("pair")
    own = lax.dynamic_slice_in_dim(block, place * size, size, axis)
    other = lax.dynamic_slice_in_dim(block, (1 - place) * size, size, axis)
    return own, other


def in_order(own, other, axis):
    place = lax.axis_index("pair")
    return jnp.where(
        place == 0,
        jnp.concatenate([own, other], axis=axis),
        jnp.concatenate([other, own], axis=axis),
    )


def after(values, earlier):
    return lax.optimization_barrier((values, earlier))[0]


def spread(block):
    return [block] + [shift(block, k) for k in range(1, HEADS)]


def collect(blocks):
    total = blocks[0].astype(jnp.float32)
    for k in range(1, HEADS):
        total = total + shift(blocks[k], -k).astype(jnp.float32)
    return total


def half_rows(block):
    own, other = halves(block, 1)
    return in_order(own, swap(other), 0)


def scatter_half(rows):
    block = collect(jnp.split(rows, HEADS, axis=1)).astype(jnp.bfloat16)
    own, other = halves(block, 0)
    return in_order(own, swap(other), 1).astype(jnp.float32)


FORWARD = [((z // 2, z), (1 - z // 2, z)) for z in range(HEADS)]


def sequence_rows(block):
    place = lax.axis_index("head")
    holds = lax.axis_index("pair") == place // 2
    inner = (place == 1) | (place == 2)
    near = send(
        block,
        [((0, 0), (0, 1)), ((0, 1), (0, 0)), ((1, 2), (1, 3)), ((1, 3), (1, 2))],
    )
    next_in = send(block, [((0, 2), (0, 1)), ((1, 1), (1, 2))])
    last_in = send(block, [((0, 3), (0, 1)), ((1, 0), (1, 2))])
    outward = [((0, 1), (0, 0)), ((1, 2), (1, 3))]
    next_out = send(next_in, outward)
    last_out = send(last_in, outward)
    pieces = (
        block,
        near,
        jnp.where(inner, next_in, next_out),
        jnp.where(inner, last_in, last_out),
    )
    passed = [send(v, FORWARD) for v in pieces]
    own, near, following, last = (jnp.where(holds, v, w) for v, w in zip(pieces, passed))
    first = jnp.where(place % 2 == 0, own, near)
    second = jnp.where(place % 2 == 0, near, own)
    low = place < 2
    joined = jnp.concatenate(
        [
            jnp.where(low, first, last),
            jnp.where(low, second, following),
            jnp.where(low, following, first),
            jnp.where(low, last, second),
        ],
        axis=0,
    )
    return joined


def sequence_sum(partial):
    place = lax.axis_index("head")
    low = place < 2
    inner = jnp.where((place == 1) | (place == 2), 1, 0)
    rows = partial.shape[0] // HEADS
    bf16 = jnp.bfloat16

    def block(i):
        index = jnp.where(low, i, HEADS - 1 - i)
        piece = lax.dynamic_slice_in_dim(partial, index * rows, rows, 0)
        own, other = lax.optimization_barrier(halves(piece, 1))
        return own.astype(jnp.float32) + swap(other).astype(jnp.float32)

    inward = both([(0, 1), (3, 2)])
    near_moves = both([(0, 1), (1, 0), (2, 3), (3, 2)])
    last = block(3)
    last_in = send(last.astype(bf16), inward)
    following = block(2)
    following_in = send(following.astype(bf16), inward)
    away_in = send(block(1 - inner).astype(bf16), near_moves)
    mine = block(inner)
    last = (last + last_in.astype(jnp.float32)).astype(bf16)
    last = send(last, both([(1, 3), (2, 0)]))
    following = (following + following_in.astype(jnp.float32)).astype(bf16)
    following = send(following, both([(1, 2), (2, 1)]))
    return mine, away_in, following, last


def sequence_end(mine, away_in, following, last):
    place = lax.axis_index("head")
    inner = (place == 1) | (place == 2)
    mine = mine + away_in.astype(jnp.float32)
    far = jnp.where(inner, following, last).astype(jnp.float32)
    keeps = lax.axis_index("pair") == place // 2
    kept = jnp.where(keeps, mine, far)
    given = swap(jnp.where(keeps, far, mine).astype(jnp.bfloat16)).astype(jnp.float32)
    return in_order(kept, given, 1)


def group_moves(k):
    moves = []
    for p in range(2):
        for z in range(HEADS):
            group = 2 * (z % 2) + p
            moves.append(((p, z), (z // 2, (group + k) % HEADS)))
    return moves


def column_moves(k):
    moves = []
    for p in range(2):
        for group in range(HEADS):
            moves.append(((p, group), (group % 2, group // 2 + 2 * (p ^ k))))
    return moves


def turned(moves):
    return [(b, a) for a, b in moves]


def group_to_rows(values):
    rows = values.shape[0] // HEADS
    group = 2 * (lax.axis_index("head") % 2) + lax.axis_index("pair")
    parts = []
    for k in range(HEADS):
        start = (group + k) % HEADS * rows
        parts.append(send(lax.dynamic_slice_in_dim(values, start, rows, 0), group_moves(k)))
    return jnp.concatenate(parts, axis=1)


def rows_to_group(values):
    odd = lax.axis_index("pair") == 1
    upper = lax.axis_index("head") % 2 == 1
    parts = [
        send(part, turned(group_moves(k)))
        for k, part in enumerate(jnp.split(values, HEADS, axis=1))
    ]
    parts = [jnp.where(odd, parts[k - 1], parts[k]) for k in range(HEADS)]
    return jnp.concatenate(
        [jnp.where(upper, parts[k - 2], parts[k]) for k in range(HEADS)], axis=0
    )


def sum_all(values):
    for axis in ALL:
        size = lax.axis_size(axis)
        step = 1
        while step < size:
            values = values + lax.ppermute(values, axis, [(i, i ^ step) for i in range(size)])
            step *= 2
    return values


def layer(
    tokens, cotangent, w_query, w_key, w_value, w_out, w_up, w_down, norm_gain, norm_bias
):
    rows = tokens.shape[0]
    width = w_query.shape[1]
    model = w_query.shape[0] * lax.axis_size("outer") * 2
    bf16 = jnp.bfloat16
    f32 = jnp.float32
    late = lax.axis_index("head") // 2
    residual = tokens.astype(f32)
    norm_a, unit_a, inv_a = normalize(residual, norm_gain[0], norm_bias[0])

    w_cols = jnp.concatenate([w_query, w_key, w_value], axis=1)
    w_first, w_second = (send(w_cols, column_moves(k)) for k in range(2))
    w_cols = jnp.where(
        late == 0,
        jnp.concatenate([w_first, w_second], axis=0),
        jnp.concatenate([w_second, w_first], axis=0),
    )
    out_parts = spread(w_out.T)
    out_low = jnp.concatenate(out_parts[: HEADS // 2], axis=1)
    out_high = jnp.concatenate(out_parts[HEADS // 2 :], axis=1)
    attention = jnp.concatenate(
        [w_cols, jnp.concatenate([out_low, out_high], axis=0)], axis=1
    )
    attention = lax.all_gather(attention, "outer", axis=0, tiled=True)
    w_cols = attention[:, : 3 * width]
    out_own = attention[:, 3 * width :].reshape(-1, 2, w_out.shape[1], 2 * width)
    out_own = jnp.concatenate([out_own[:, 0], out_own[:, 1]], axis=2)
    seq_a = sequence_rows(norm_a.astype(bf16))
    up_block = half_rows(w_up)
    up_parts = spread(up_block)
    up_parts = jnp.concatenate(up_parts, axis=1)
    full_up = lax.all_gather(up_parts, "outer", axis=0, tiled=True)
    down_block = half_rows(w_down.T)
    down_parts = spread(down_block)

    block_rows = min(512, seq_a.shape[0])
    qkv = jnp.dot(seq_a, w_cols, preferred_element_type=f32).astype(bf16)
    down_parts = jnp.concatenate(down_parts, axis=1)
    full_down = lax.all_gather(down_parts, "outer", axis=0, tiled=True)
    queries, key_rows, value_rows = (qkv[:, i * width : (i + 1) * width] for i in range(3))
    attended, totals = attend(queries, key_rows, value_rows, block_rows)
    attended = group_to_rows(attended.astype(bf16))
    out_other = swap(out_own)
    place = lax.axis_index("pair")
    full_o = jnp.stack(
        [jnp.where(place == 0, out_own, out_other), jnp.where(place == 0, out_other, out_own)],
        axis=1,
    ).reshape(model, -1)
    mixed = contract_cols(attended, full_o)
    norm_z, unit_z, inv_z = normalize(mixed, norm_gain[1], norm_bias[1])
    hidden = residual + norm_z
    norm_c, unit_c, inv_c = normalize(hidden, norm_gain[2], norm_bias[2])
    rows_c = norm_c.astype(bf16)
    pair_c = jnp.concatenate([rows_c, swap(rows_c)], axis=0)
    pre_act = jnp.dot(pair_c, full_up, preferred_element_type=f32)
    active, gelu_back = jax.vjp(jax.nn.gelu, pre_act)
    active = active.astype(bf16)
    both_m = contract_cols(active, full_down)
    output = both_m[:rows] + swap(both_m[rows:].astype(bf16)).astype(f32)
    norm_m, unit_m, inv_m = normalize(output, norm_gain[3], norm_bias[3])
    block_out = (hidden + norm_m).astype(bf16)

    grad_y = cotangent.astype(f32)
    grad_m, gain_m, bias_m = normalize_back(grad_y, unit_m, inv_m, norm_gain[3])
    rows_gm = grad_m.astype(bf16)
    pair_gm = jnp.concatenate([rows_gm, swap(rows_gm)], axis=0)
    grad_act = jnp.dot(pair_gm, full_down, preferred_element_type=f32)
    grad_pre = gelu_back(grad_act)[0].astype(bf16)
    both_c = contract_cols(grad_pre, full_up)
    grad_c = both_c[:rows] + swap(both_c[rows:].astype(bf16)).astype(f32)
    grad_down = contract_rows(pair_gm, active).astype(bf16)
    grad_up = contract_rows(pair_c, grad_pre).astype(bf16)
    grad_more, gain_c, bias_c = normalize_back(grad_c, unit_c, inv_c, norm_gain[2])
    grad_h = grad_y + grad_more
    grad_z, gain_z, bias_z = normalize_back(grad_h, unit_z, inv_z, norm_gain[1])
    rows_gz = grad_z.astype(bf16)
    grad_att = jnp.dot(rows_gz, full_o, preferred_element_type=f32).astype(bf16)
    grad_att = rows_to_group(grad_att)
    grad_o = contract_rows(rows_gz, attended).astype(bf16)
    grad_o = grad_o.reshape(-1, 2, w_out.shape[1], attended.shape[1])
    own_o, other_o = halves(grad_o, 1)
    grad_o = (own_o.astype(f32) + swap(other_o).astype(f32)).astype(bf16)
    grad_o = grad_o.reshape(-1, attended.shape[1])
    grad_att = after(grad_att, (grad_down, grad_up, grad_o))
    grad_down = lax.psum_scatter(grad_down, "outer", scatter_dimension=0, tiled=True)
    grad_up = lax.psum_scatter(grad_up, "outer", scatter_dimension=0, tiled=True)
    grad_queries, grad_keys, grad_values = attend_back(
        queries, key_rows, value_rows, grad_att, totals, block_rows, (grad_down, grad_up)
    )
    grad_down = scatter_half(grad_down).T
    grad_up = scatter_half(grad_up)
    grad_qkv = jnp.concatenate([grad_queries, grad_keys, grad_values], axis=1)
    grad_qkv = after(grad_qkv, (grad_down, grad_up))
    grad_a = contract_cols(grad_qkv, w_cols).astype(bf16)
    grad_w = contract_rows(seq_a, after(grad_qkv, grad_a)).astype(bf16)
    grad_a = sequence_sum(grad_a)
    grad_o = grad_o.reshape(-1, 1, w_out.shape[1], attended.shape[1])
    grad_o = jnp.concatenate(jnp.split(grad_o, 2, axis=3), axis=1).reshape(model, -1)
    grad_w = jnp.concatenate([grad_w, grad_o], axis=1)
    grad_w = lax.psum_scatter(grad_w, "outer", scatter_dimension=0, tiled=True)
    landed = grad_w
    grad_w, grad_o = grad_w[:, : 3 * width], grad_w[:, 3 * width :]
    grad_o = collect(
        [
            grad_o[i * w_out.shape[1] : (i + 1) * w_out.shape[1], j * width : (j + 1) * width]
            for i in range(2)
            for j in range(2)
        ]
    ).T
    size = grad_w.shape[0] // 2
    parts = [
        send(
            lax.dynamic_slice_in_dim(grad_w, jnp.where(late == k, 0, size), size, 0),
            turned(column_moves(k)),
        ).astype(f32)
        for k in range(2)
    ]
    grad_w = parts[0] + parts[1]
    grad_a = sequence_end(*grad_a[:2], *after(grad_a[2:], landed))
    grad_first, gain_a, bias_a = normalize_back(grad_a, unit_a, inv_a, norm_gain[0])
    input_grad = grad_h + grad_first
    sums = sum_all(jnp.stack([gain_a, gain_z, gain_c, gain_m, bias_a, bias_z, bias_c, bias_m]))
    return (
        block_out,
        input_grad,
        grad_w[:, :width],
        grad_w[:, width : 2 * width],
        grad_w[:, 2 * width :],
        grad_o,
        grad_up,
        grad_down,
        sums[:4],
        sums[4:],
    )


def solution(mesh):
    wide, head = mesh.shape["wide"], mesh.shape["head"]
    assert head == HEADS and wide % 2 == 0
    paired = Mesh(mesh.devices.reshape(wide // 2, 2, head), ALL)
    rows = P(ALL, None)
    by_rows = P(WIDE, "head")
    by_cols = P("head", WIDE)
    in_specs = (rows, rows, by_rows, by_rows, by_rows, by_cols, by_rows, by_cols, P(), P())
    out_specs = (rows, rows, by_rows, by_rows, by_rows, by_cols, by_rows, by_cols, P(), P())
    return jax.shard_map(
        layer, mesh=paired, in_specs=in_specs, out_specs=out_specs, check_vma=False
    )
```

profile of v0, /device:TPU:0, one launch (start us, length us, event | category | flops | bytes accessed | tf_op | source)
XLA Modules:
  0.0 584.7 jit_solution(1272530326694369750)
XLA Ops:
  20.6 8.8 %collective-permute-done.12 = bf16[128,256]{1,0:T(8,128)(2,1)S(1)} collective-permute-done((bf16[128,256]{1,0:T(8,128)(2,1)S(1)}, bf16[128,256]{1,0:T(8,128)(2,1)S(1)}, u32[]{:S(2)}, u32[]{:S(2)}) %collective-permute-start.12) | collective-permute-done | bytes 65568 | tf_op jit(solution)/shard_map/ppermute | solution.py:154
  42.5 15.3 %collective-permute-done.22 = bf16[256,512]{0,1:T(8,128)(2,1)S(1)} collective-permute-done((bf16[256,512]{0,1:T(8,128)(2,1)S(1)}, bf16[256,512]{0,1:T(8,128)(2,1)S(1)}, u32[]{:S(2)}, u32[]{:S(2)}) %collective-permute-start.22) | collective-permute-done | bytes 262176 | tf_op jit(solution)/shard_map/ppermute | solution.py:154
  77.7 11.2 %collective-permute-done.1 = bf16[512,1024]{1,0:T(8,128)(2,1)} collective-permute-done((bf16[512,1024]{1,0:T(8,128)(2,1)}, bf16[512,1024]{1,0:T(8,128)(2,1)}, u32[]{:S(2)}, u32[]{:S(2)}) %collective-permute-start.1) | collective-permute-done | bytes 1048608 | tf_op jit(solution)/shard_map/ppermute | solution.py:146
  88.8 6.9 %collective-permute-start.2 = (bf16[512,1024]{1,0:T(8,128)(2,1)}, bf16[512,1024]{1,0:T(8,128)(2,1)}, u32[]{:S(2)}, u32[]{:S(2)}) collective-permute-start(bf16[512,1024]{1,0:T(8,128)(2,1)} %collective-permute-done.1), channel_id=1, source_target_pairs={{0,4},{1,5},{6,2},{7,3},{8,12},{9,13},{14,10},{15,11},{16,20},{17,... | collective-permute-start | bytes 3145736 | tf_op jit(solution)/shard_map/ppermute | solution.py:146
  95.7 8.5 %collective-permute-done.4 = bf16[512,1024]{1,0:T(8,128)(2,1)} collective-permute-done((bf16[512,1024]{1,0:T(8,128)(2,1)}, bf16[512,1024]{1,0:T(8,128)(2,1)}, u32[]{:S(2)}, u32[]{:S(2)}) %collective-permute-start.4) | collective-permute-done | bytes 1048608 | tf_op jit(solution)/shard_map/ppermute | solution.py:146
  109.8 7.1 %collective-permute-done.7 = bf16[512,1024]{1,0:T(8,128)(2,1)} collective-permute-done((bf16[512,1024]{1,0:T(8,128)(2,1)}, bf16[512,1024]{1,0:T(8,128)(2,1)}, u32[]{:S(2)}, u32[]{:S(2)}) %collective-permute-start.7) | collective-permute-done | bytes 1048608 | tf_op jit(solution)/shard_map/ppermute | solution.py:146
  119.6 17.5 %collective-permute-done.26 = bf16[256,512]{0,1:T(8,128)(2,1)S(1)} collective-permute-done((bf16[256,512]{0,1:T(8,128)(2,1)S(1)}, bf16[256,512]{0,1:T(8,128)(2,1)S(1)}, u32[]{:S(2)}, u32[]{:S(2)}) %collective-permute-start.26) | collective-permute-done | bytes 262176 | tf_op jit(solution)/shard_map/ppermute | solution.py:154
  188.9 7.3 %fusion.108 = bf16[512,4,64]{0,2,1:T(8,128)(2,1)} fusion(bf16[2048,4,64]{0,2,1:T(8,128)(2,1)} %bitcast.184, f32[4,512,2048]{2,1,0:T(8,128)S(1)} %get-tuple-element.297, f32[4,512]{1,0:T(4,128)S(1)} %fusion.1, f32[4,512]{1,0:T(4,128)S(1)} %get-tuple-element.296, pred[512,2048]{1,0:T(8,128)(4,1)S(1)} %iota_compare_fusion), kind=kOutput, calls=%fused_computation.166 | convolution fusion | flops 557973504 | bytes 19152896 | tf_op jit(solution)/shard_map/gqk,kgd->qgd/dot_general | solution.py:64
  231.3 10.4 %fusion.87 = f32[1024,2048]{1,0:T(8,128)} fusion(bf16[1024,2048]{0,1:T(8,128)(2,1)} %all-gather.6.cloned.1.call-done, bf16[512,1024]{1,0:T(8,128)(2,1)} %collective-permute-done.19, bf16[512,1024]{1,0:T(8,128)(2,1)S(1)} %add_convert_fusion.2), kind=kOutput, calls=%fused_computation.144 | convolution fusion | flops 4299161600 | bytes 14680064 | tf_op jit(solution)/shard_map/dot_general | solution.py:388
  241.7 9.2 %fusion.133 = f32[1024,1024]{1,0:T(8,128)S(1)} fusion(bf16[1024,2048]{0,1:T(8,128)(2,1)} %all-gather.8.cloned.1.call-done, f32[1024,2048]{1,0:T(8,128)} %fusion.87), kind=kOutput, calls=%fused_computation.286 | convolution fusion | flops 4313841664 | bytes 16777216 | tf_op jit(solution)/shard_map/dot_general | solution.py:130
  268.1 12.8 %fusion.11 = bf16[1024,2048]{1,0:T(8,128)(2,1)S(1)} fusion(f32[1024,2048]{1,0:T(8,128)} %fusion.87, bf16[1024,2048]{0,1:T(8,128)(2,1)} %all-gather.8.cloned.1.call-done, bf16[512,1024]{1,0:T(8,128)(2,1)} %copy-done.84, bf16[512,1024]{1,0:T(8,128)(2,1)} %copy-done.58), kind=kOutput, calls=%fused_computation.25 | convolution fusion | flops 4341104640 | bytes 18874368 | tf_op jit(solution)/shard_map/dot_general | solution.py:400
  288.9 7.4 %convolution_convert_fusion.1 = bf16[1024,2048]{1,0:T(8,128)(2,1)} fusion(bf16[1024,2048]{1,0:T(8,128)(2,1)S(1)} %fusion.11, bf16[512,1024]{1,0:T(8,128)(2,1)} %collective-permute-done.19, bf16[512,1024]{1,0:T(8,128)(2,1)S(1)} %copy-done.63), kind=kOutput, calls=%fused_computation.53 | convolution fusion | flops 4301258752 | bytes 10485760 | tf_op jit(solution)/shard_map/dot_general | solution.py:124
  320.6 7.2 %collective-permute-done.33 = bf16[512,256]{1,0:T(8,128)(2,1)S(1)} collective-permute-done((bf16[512,256]{1,0:T(8,128)(2,1)S(1)}, bf16[512,256]{1,0:T(8,128)(2,1)S(1)}, u32[]{:S(2)}, u32[]{:S(2)}) %collective-permute-start.33) | collective-permute-done | bytes 262176 | tf_op jit(solution)/shard_map/ppermute | solution.py:146
  327.8 9.1 %collective-permute-done.32 = bf16[512,256]{1,0:T(8,128)(2,1)S(1)} collective-permute-done((bf16[512,256]{1,0:T(8,128)(2,1)S(1)}, bf16[512,256]{1,0:T(8,128)(2,1)S(1)}, u32[]{:S(2)}, u32[]{:S(2)}) %collective-permute-start.32) | collective-permute-done | bytes 262176 | tf_op jit(solution)/shard_map/ppermute | solution.py:146
  356.5 8.1 %multiply_reduce_fusion.2 = (f32[4,512]{1,0:T(4,128)S(1)}, f32[4,512,1024]{2,1,0:T(8,128)}) fusion(f32[4,512,1024]{2,1,0:T(8,128)} %copy-done.1, f32[4,512]{1,0:T(4,128)S(1)} %log_add_fusion.2, bf16[512,4,64]{0,2,1:T(8,128)(2,1)S(1)} %bitcast.198, bf16[1024,4,64]{0,2,1:T(8,128)(2,1)S(1)} %bitcast.211), kind=kOutput, calls=%fused_computation.27 | convolution fusion | flops 274724864 | bytes 17580032 | tf_op jit(solution)/shard_map/qgd,kgd->gqk/dot_general | solution.py:97
  372.4 8.5 %multiply_reduce_fusion.1 = (f32[4,512]{1,0:T(4,128)S(1)}, f32[4,512,1536]{2,1,0:T(8,128)}) fusion(f32[4,512,1536]{2,1,0:T(8,128)S(1)} %bitcast.170, f32[4,512]{1,0:T(4,128)S(1)} %log_add_fusion.1, bf16[512,4,64]{0,2,1:T(8,128)(2,1)} %bitcast.194, bf16[1536,4,64]{0,2,1:T(8,128)(2,1)} %bitcast.193), kind=kOutput, calls=%fused_computation.9 | convolution fusion | flops 412088320 | bytes 26230784 | tf_op jit(solution)/shard_map/qgd,kgd->gqk/dot_general | solution.py:97
  416.8 11.5 %multiply_reduce_fusion = (f32[4,512]{1,0:T(4,128)}, f32[4,512,2048]{2,1,0:T(8,128)}) fusion(f32[4,512,2048]{2,1,0:T(8,128)S(1)} %fusion.156, f32[4,512]{1,0:T(4,128)S(1)} %log_add_fusion, pred[512,2048]{1,0:T(8,128)(4,1)S(1)} %copy-done.8, bf16[2048,4,64]{0,2,1:T(8,128)(2,1)} %bitcast.185, bf16[2048,4,64]{0,2,1:T(8,128)(2,1)} %bitcast.212), kind=kOutput, calls=%fused_computation.1 | convolution fusion | flops 557840384 | bytes 35930112 | tf_op jit(solution)/shard_map/qgd,kgd->gqk/dot_general | solution.py:97
  428.3 7.4 %fusion.51 = bf16[2048,4,64]{0,2,1:T(8,128)(2,1)} fusion(f32[2048,4,64]{0,2,1:T(8,128)} %fusion.45, f32[4,512,2048]{2,1,0:T(8,128)S(1)} %fusion.156, f32[4,512]{1,0:T(4,128)S(1)} %log_add_fusion, pred[512,2048]{1,0:T(8,128)(4,1)S(1)} %copy-done.8, bf16[2048,4,64]{0,2,1:T(8,128)(2,1)} %bitcast.213), kind=kOutput, calls=%fused_computation.83 | convolution fusion | flops 554696704 | bytes 21241856 | tf_op jit(solution)/shard_map/gqk,qgd->kgd/dot_general | solution.py:95
  435.7 8.4 %multiply_convert_fusion = bf16[4,512,2048]{2,1,0:T(8,128)(2,1)S(1)} fusion(f32[4,512,2048]{2,1,0:T(8,128)} %get-tuple-element.313, f32[4,512,2048]{2,1,0:T(8,128)S(1)} %fusion.156, f32[4,512]{1,0:T(4,128)S(1)} %copy-done.80, f32[4,512]{1,0:T(4,128)S(1)} %log_add_fusion, pred[512,2048]{1,0:T(8,128)(4,1)S(1)} %copy-done.8), kind=kLoop, calls=%fused_computation | loop fusion | flops 25165824 | bytes 43008000 | tf_op jit(solution)/shard_map/convert_element_type | solution.py:101
  453.8 9.3 %collective-permute-done.40 = bf16[256,512]{1,0:T(8,128)(2,1)S(1)} collective-permute-done((bf16[256,512]{1,0:T(8,128)(2,1)S(1)}, bf16[256,512]{1,0:T(8,128)(2,1)S(1)}, u32[]{:S(2)}, u32[]{:S(2)}) %collective-permute-start.40) | collective-permute-done | bytes 262176 | tf_op jit(solution)/shard_map/ppermute | solution.py:154
  489.3 10.2 %collective-permute-done.47 = bf16[512,512]{1,0:T(8,128)(2,1)S(1)} collective-permute-done((bf16[512,512]{1,0:T(8,128)(2,1)S(1)}, bf16[512,512]{1,0:T(8,128)(2,1)S(1)}, u32[]{:S(2)}, u32[]{:S(2)}) %collective-permute-start.47) | collective-permute-done | bytes 524320 | tf_op jit(solution)/shard_map/ppermute | solution.py:146
  501.1 8.8 %collective-permute-done.50 = bf16[512,512]{1,0:T(8,128)(2,1)S(1)} collective-permute-done((bf16[512,512]{1,0:T(8,128)(2,1)S(1)}, bf16[512,512]{1,0:T(8,128)(2,1)S(1)}, u32[]{:S(2)}, u32[]{:S(2)}) %collective-permute-start.50) | collective-permute-done | bytes 524320 | tf_op jit(solution)/shard_map/ppermute | solution.py:146
  518.6 9.9 %collective-permute-done.51 = bf16[512,512]{1,0:T(8,128)(2,1)} collective-permute-done((bf16[512,512]{1,0:T(8,128)(2,1)}, bf16[512,512]{1,0:T(8,128)(2,1)}, u32[]{:S(2)}, u32[]{:S(2)}) %collective-permute-start.51) | collective-permute-done | bytes 524320 | tf_op jit(solution)/shard_map/ppermute | solution.py:146
  528.5 11.1 %collective-permute-done.45 = bf16[512,512]{1,0:T(8,128)(2,1)} collective-permute-done((bf16[512,512]{1,0:T(8,128)(2,1)}, bf16[512,512]{1,0:T(8,128)(2,1)}, u32[]{:S(2)}, u32[]{:S(2)}) %collective-permute-start.45) | collective-permute-done | bytes 524320 | tf_op jit(solution)/shard_map/ppermute | solution.py:146
  (487 shorter events, 336.6 us)
Async XLA Ops:
  7.2 143.4 %all-gather.4.cloned.1.call-start = ((), (), s32[]{:S(2)}) async-start(), calls=%async_computation.3 | async-start | bytes 3276800 | tf_op jit(solution)/shard_map/all_gather | solution.py:357
  30.3 201.0 %all-gather.6.cloned.1.call-start = ((), (), s32[]{:S(2)}) async-start(), calls=%async_computation.4 | async-start | bytes 5242880 | tf_op jit(solution)/shard_map/all_gather | solution.py:365
  34.3 23.5 %collective-permute-start.22 = (bf16[256,512]{0,1:T(8,128)(2,1)S(1)}, bf16[256,512]{0,1:T(8,128)(2,1)S(1)}, u32[]{:S(2)}, u32[]{:S(2)}) collective-permute-start(bf16[256,512]{0,1:T(8,128)(2,1)S(1)} %maximum_select_fusion.2), channel_id=1, source_target_pairs={{0,2},{1,3},{2,0},{3,1},{4,6},{5,7},{6,4},{7,5},{8,10},{9,11},{10,... | collective-permute-start | bytes 786440 | tf_op jit(solution)/shard_map/ppermute | solution.py:154
  58.8 182.9 %all-gather.8.cloned.1.call-start = ((), (), s32[]{:S(2)}) async-start(), calls=%async_computation.5 | async-start | bytes 5242880 | tf_op jit(solution)/shard_map/all_gather | solution.py:372
  64.3 24.5 %collective-permute-start.1 = (bf16[512,1024]{1,0:T(8,128)(2,1)}, bf16[512,1024]{1,0:T(8,128)(2,1)}, u32[]{:S(2)}, u32[]{:S(2)}) collective-permute-start(bf16[512,1024]{1,0:T(8,128)(2,1)} %fusion.62), channel_id=1, source_target_pairs={{0,1},{1,0},{6,7},{7,6},{8,9},{9,8},{14,15},{15,14},{16,17},{17,16... | collective-permute-start | bytes 3145736 | tf_op jit(solution)/shard_map/ppermute | solution.py:146
  66.5 76.3 %collective-permute-start = (bf16[512,1024]{1,0:T(8,128)(2,1)}, bf16[512,1024]{1,0:T(8,128)(2,1)}, u32[]{:S(2)}, u32[]{:S(2)}) collective-permute-start(bf16[512,1024]{1,0:T(8,128)(2,1)} %fusion.62), channel_id=1, source_target_pairs={{0,4},{1,5},{6,2},{7,3},{8,12},{9,13},{14,10},{15,11},{16,20},{17,... | collective-permute-start | bytes 3145736 | tf_op jit(solution)/shard_map/ppermute | solution.py:146
  72.9 36.7 %collective-permute-start.24 = (bf16[128,512]{0,1:T(8,128)(2,1)S(1)}, bf16[128,512]{0,1:T(8,128)(2,1)S(1)}, u32[]{:S(2)}, u32[]{:S(2)}) collective-permute-start(bf16[128,512]{0,1:T(8,128)(2,1)S(1)} %get-tuple-element.285), channel_id=1, source_target_pairs={{0,4},{4,0},{1,5},{5,1},{2,6},{6,2},{3,7},{7,3},{8,12},{12,8},{9,1... | collective-permute-start | bytes 393224 | tf_op jit(solution)/shard_map/ppermute | solution.py:142
  73.0 31.3 %collective-permute-start.4 = (bf16[512,1024]{1,0:T(8,128)(2,1)}, bf16[512,1024]{1,0:T(8,128)(2,1)}, u32[]{:S(2)}, u32[]{:S(2)}) collective-permute-start(bf16[512,1024]{1,0:T(8,128)(2,1)} %collective-permute-done.3), channel_id=1, source_target_pairs={{1,0},{6,7},{9,8},{14,15},{17,16},{22,23},{25,24},{30,31}} | collective-permute-start | bytes 3145736 | tf_op jit(solution)/shard_map/ppermute | solution.py:146
  75.7 41.1 %collective-permute-start.7 = (bf16[512,1024]{1,0:T(8,128)(2,1)}, bf16[512,1024]{1,0:T(8,128)(2,1)}, u32[]{:S(2)}, u32[]{:S(2)}) collective-permute-start(bf16[512,1024]{1,0:T(8,128)(2,1)} %collective-permute-done.6), channel_id=1, source_target_pairs={{1,0},{6,7},{9,8},{14,15},{17,16},{22,23},{25,24},{30,31}} | collective-permute-start | bytes 3145736 | tf_op jit(solution)/shard_map/ppermute | solution.py:146
  88.8 54.0 %collective-permute-start.2 = (bf16[512,1024]{1,0:T(8,128)(2,1)}, bf16[512,1024]{1,0:T(8,128)(2,1)}, u32[]{:S(2)}, u32[]{:S(2)}) collective-permute-start(bf16[512,1024]{1,0:T(8,128)(2,1)} %collective-permute-done.1), channel_id=1, source_target_pairs={{0,4},{1,5},{6,2},{7,3},{8,12},{9,13},{14,10},{15,11},{16,20},{17,... | collective-permute-start | bytes 3145736 | tf_op jit(solution)/shard_map/ppermute | solution.py:146
  106.5 36.3 %collective-permute-start.5 = (bf16[512,1024]{1,0:T(8,128)(2,1)}, bf16[512,1024]{1,0:T(8,128)(2,1)}, u32[]{:S(2)}, u32[]{:S(2)}) collective-permute-start(bf16[512,1024]{1,0:T(8,128)(2,1)} %broadcast_select_fusion.1), channel_id=1, source_target_pairs={{0,4},{1,5},{6,2},{7,3},{8,12},{9,13},{14,10},{15,11},{16,20},{17,... | collective-permute-start | bytes 3145736 | tf_op jit(solution)/shard_map/ppermute | solution.py:146
  142.3 262.3 %reduce-scatter.4.cloned.1.call-start = ((), (), s32[]{:S(2)}) async-start(), calls=%async_computation.6 | async-start | bytes 5242880 | tf_op jit(solution)/shard_map/reduce_scatter | solution.py:418
  161.0 57.1 %collective-permute-start.18 = (bf16[4,128,1024]{2,1,0:T(8,128)(2,1)}, bf16[4,128,1024]{2,1,0:T(8,128)(2,1)}, u32[]{:S(2)}, u32[]{:S(2)}) collective-permute-start(bf16[4,128,1024]{2,1,0:T(8,128)(2,1)} %pad_maximum_fusion.13), channel_id=1, source_target_pairs={{0,4},{4,0},{1,5},{5,1},{2,6},{6,2},{3,7},{7,3},{8,12},{12,8},{9,1... | collective-permute-start | bytes 3145736 | tf_op jit(solution)/shard_map/ppermute | solution.py:142
  268.0 140.6 %reduce-scatter.6.cloned.1.call-start = ((), (), s32[]{:S(2)}) async-start(), calls=%async_computation.7 | async-start | bytes 5242880 | tf_op jit(solution)/shard_map/reduce_scatter | solution.py:419
  296.3 232.2 %reduce-scatter.8.cloned.1.call-start = ((), (), s32[]{:S(2)}) async-start(), calls=%async_computation.8 | async-start | bytes 3276800 | tf_op jit(solution)/shard_map/reduce_scatter | solution.py:433
  319.3 82.1 %collective-permute-start.52 = (bf16[4,1,128,1024]{3,2,1,0:T(8,128)(2,1)}, bf16[4,1,128,1024]{3,2,1,0:T(8,128)(2,1)}, u32[]{:S(2)}, u32[]{:S(2)}) collective-permute-start(bf16[4,1,128,1024]{3,2,1,0:T(8,128)(2,1)} %constant_dynamic-slice_fusion.2), channel_id=1, source_target_pairs={{0,4},{4,0},{1,5},{5,1},{2,6},{6,2},{3,7},{7,3},{8,12},{12,8},{9,1... | collective-permute-start | bytes 3145736 | tf_op jit(solution)/shard_map/ppermute | solution.py:142
  406.6 43.1 %collective-permute-start.35 = (bf16[256,512]{1,0:T(8,128)(2,1)}, bf16[256,512]{1,0:T(8,128)(2,1)}, u32[]{:S(2)}, u32[]{:S(2)}) collective-permute-start(bf16[256,512]{1,0:T(8,128)(2,1)} %get-tuple-element.250), channel_id=1, source_target_pairs={{0,3},{1,0},{2,1},{3,2},{4,7},{5,4},{6,5},{7,6},{8,11},{9,8},{10,9... | collective-permute-start | bytes 786440 | tf_op jit(solution)/shard_map/ppermute | solution.py:154
  406.6 45.8 %collective-permute-start.37 = (bf16[256,512]{1,0:T(8,128)(2,1)}, bf16[256,512]{1,0:T(8,128)(2,1)}, u32[]{:S(2)}, u32[]{:S(2)}) collective-permute-start(bf16[256,512]{1,0:T(8,128)(2,1)} %get-tuple-element.251), channel_id=1, source_target_pairs={{0,1},{1,2},{2,3},{3,0},{4,5},{5,6},{6,7},{7,4},{8,9},{9,10},{10,1... | collective-permute-start | bytes 786440 | tf_op jit(solution)/shard_map/ppermute | solution.py:154
  408.6 43.7 %collective-permute-start.36 = (bf16[256,512]{1,0:T(8,128)(2,1)}, bf16[256,512]{1,0:T(8,128)(2,1)}, u32[]{:S(2)}, u32[]{:S(2)}) collective-permute-start(bf16[256,512]{1,0:T(8,128)(2,1)} %get-tuple-element.252), channel_id=1, source_target_pairs={{0,2},{1,3},{2,0},{3,1},{4,6},{5,7},{6,4},{7,5},{8,10},{9,11},{10,... | collective-permute-start | bytes 786440 | tf_op jit(solution)/shard_map/ppermute | solution.py:154
  410.6 43.2 %collective-permute-start.39 = (bf16[256,512]{1,0:T(8,128)(2,1)}, bf16[256,512]{1,0:T(8,128)(2,1)}, u32[]{:S(2)}, u32[]{:S(2)}) collective-permute-start(bf16[256,512]{1,0:T(8,128)(2,1)} %get-tuple-element.247), channel_id=1, source_target_pairs={{0,3},{1,0},{2,1},{3,2},{4,7},{5,4},{6,5},{7,6},{8,11},{9,8},{10,9... | collective-permute-start | bytes 786440 | tf_op jit(solution)/shard_map/ppermute | solution.py:154
  413.0 40.8 %collective-permute-start.41 = (bf16[256,512]{1,0:T(8,128)(2,1)}, bf16[256,512]{1,0:T(8,128)(2,1)}, u32[]{:S(2)}, u32[]{:S(2)}) collective-permute-start(bf16[256,512]{1,0:T(8,128)(2,1)} %get-tuple-element.248), channel_id=1, source_target_pairs={{0,1},{1,2},{2,3},{3,0},{4,5},{5,6},{6,7},{7,4},{8,9},{9,10},{10,1... | collective-permute-start | bytes 786440 | tf_op jit(solution)/shard_map/ppermute | solution.py:154
  488.7 39.8 %collective-permute-start.43 = (bf16[512,512]{1,0:T(8,128)(2,1)S(1)}, bf16[512,512]{1,0:T(8,128)(2,1)S(1)}, u32[]{:S(2)}, u32[]{:S(2)}) collective-permute-start(bf16[512,512]{1,0:T(8,128)(2,1)S(1)} %get-tuple-element.142), channel_id=1, source_target_pairs={{0,4},{4,0},{1,5},{5,1},{2,6},{6,2},{3,7},{7,3},{8,12},{12,8},{9,1... | collective-permute-start | bytes 1572872 | tf_op jit(solution)/shard_map/ppermute | solution.py:142
  488.8 23.5 %collective-permute-start.44 = (bf16[512,512]{1,0:T(8,128)(2,1)S(1)}, bf16[512,512]{1,0:T(8,128)(2,1)S(1)}, u32[]{:S(2)}, u32[]{:S(2)}) collective-permute-start(bf16[512,512]{1,0:T(8,128)(2,1)S(1)} %get-tuple-element.144), channel_id=1, source_target_pairs={{0,4},{4,0},{1,5},{5,1},{2,6},{6,2},{3,7},{7,3},{8,12},{12,8},{9,1... | collective-permute-start | bytes 1572872 | tf_op jit(solution)/shard_map/ppermute | solution.py:142
  513.2 26.4 %collective-permute-start.45 = (bf16[512,512]{1,0:T(8,128)(2,1)}, bf16[512,512]{1,0:T(8,128)(2,1)}, u32[]{:S(2)}, u32[]{:S(2)}) collective-permute-start(bf16[512,512]{1,0:T(8,128)(2,1)} %add_convert_fusion.5), channel_id=1, source_target_pairs={{0,1},{1,0},{2,3},{3,2},{4,5},{5,4},{6,7},{7,6},{8,9},{9,8},{10,11... | collective-permute-start | bytes 1572872 | tf_op jit(solution)/shard_map/ppermute | solution.py:146
  (140 other events, 1716.7 us)
Sparse Core Ops, SparseCore 0:
  30.4 38.4 all-gather.3
  70.7 52.4 all-gather.5
  142.4 50.6 all-gather.7
  268.1 51.4 reduce-scatter.3
  322.4 52.5 reduce-scatter.5
  477.7 39.5 reduce-scatter.7
where the time goes:
time: 591 us; the launch traced here: 585 us
  waiting for transfers between devices  164 us (28%)
  matrix products  159 us (27%)
  starting transfers between devices  101 us (17%)
  other arithmetic  93.2 us (16%)
  local copies, waits for them, and re-layouts  50.5 us (9%)
  between operations  16.2 us (3%)
    ppermute x26, waiting for transfers between devices, send(): lax.ppermute(values, LINE, [(a * HEADS + b, c * HEADS + d) for (a, b), (c...  93.1 us
    ppermute x26, starting transfers between devices, send(): lax.ppermute(values, LINE, [(a * HEADS + b, c * HEADS + d) for (a, b), (c...  67.4 us
    ppermute x18, waiting for transfers between devices, shift(): lax.ppermute(values, 'head', [(i, (i + step) % HEADS) for i in range(HEAD...  58.3 us
    dot_general x4, matrix products, attend_back(): jnp.einsum('qgd,kgd->gqk', grad_block, value_heads[:last_row], preferred_...  31.5 us
    convert_element_type x4, other arithmetic, attend_back(): grad_scores = (weights * (grad_weights - inner_sum)).astype(jnp.bfloat16)  20.6 us
    dot_general x4, matrix products, contract_cols(): lax.dot_general(left_op, right_op, (((1,), (1,)), ((), ())), preferred_el...  20.5 us
    unnamed x196, local copies, waits for them, and re-layouts  19.5 us
    dot_general x4, matrix products, contract_rows(): lax.dot_general(left_op, right_op, (((0,), (0,)), ((), ())), preferred_el...  18.8 us
  transfers between devices with their start and end apart: 70, of which 28 were waited for; matrix products, arithmetic and copies ran while one was open for 43% of the time, Pallas kernels for 0%

commit v1 on v0

--- a/solution.py
+++ b/solution.py
@@ -3,6 +3,8 @@
 import jax
 import jax.numpy as jnp
 from jax import lax
+from jax.experimental import pallas as pl
+from jax.experimental.pallas import tpu as pltpu
 from jax.sharding import Mesh, PartitionSpec as P
 
 
@@ -30,94 +32,181 @@
     return (inner_sum * inverse, jnp.sum(gradient * unit_rows, axis=0), jnp.sum(gradient, axis=0))
 
 
-def masked_scores(rows_q, key_heads, first_row, score_scale):
-    scores = (
-        jnp.einsum("qgd,kgd->gqk", rows_q, key_heads, preferred_element_type=jnp.float32)
-        * score_scale
-    )
-    place_q = first_row + jnp.arange(rows_q.shape[0], dtype=jnp.int32)
-    place_k = jnp.arange(key_heads.shape[0], dtype=jnp.int32)
-    allowed = place_k[None, :] <= place_q[:, None]
-    return jnp.where(allowed[None], scores, -1e30)
-
-
-def attend(queries, key_rows, value_rows, block_rows):
-    length, width = queries.shape
-    groups = width // HD
+def head_lanes(shape, head):
+    lane = lax.broadcasted_iota(jnp.int32, shape, 1)
+    return (lane >= head * HD) & (lane < (head + 1) * HD)
+
+
+def causal(shape):
+    key = lax.broadcasted_iota(jnp.int32, shape, 0)
+    query = lax.broadcasted_iota(jnp.int32, shape, 1)
+    return key <= query
+
+
+NT = (((1,), (1,)), ((), ()))
+
+
+def attend_kernel(q_ref, k_ref, vt_ref, out_ref, total_ref, acc_ref):
+    block, width = q_ref.shape
+    position = pl.program_id(0)
+    scaled = q_ref[...] * jnp.asarray(1.0 / math.sqrt(HD), jnp.bfloat16)
+    heads = [
+        jnp.where(head_lanes((block, width), h), scaled, jnp.zeros_like(scaled))
+        for h in range(width // HD)
+    ]
+
+    def scores(h, j):
+        start = pl.multiple_of(j * block, block)
+        keys = k_ref[pl.ds(start, block), :]
+        return lax.dot_general(keys, heads[h], NT, preferred_element_type=jnp.float32)
+
+    def mix(h, j, weights):
+        start = pl.multiple_of(j * block, block)
+        values = vt_ref[h * HD : (h + 1) * HD, pl.ds(start, block)]
+        return jnp.dot(values, weights.astype(jnp.bfloat16), preferred_element_type=jnp.float32)
+
+    first = []
+    for h in range(width // HD):
+        s = jnp.where(causal((block, block)), scores(h, position), -1e30)
+        top = jnp.max(s, axis=0, keepdims=True)
+        p = jnp.exp(s - top)
+        first += [top, jnp.sum(p, axis=0, keepdims=True)]
+        acc_ref[h * HD : (h + 1) * HD, :] = mix(h, position, p)
+
+    def step(j, carry):
+        carry = list(carry)
+        for h in range(width // HD):
+            s = scores(h, j)
+            top = jnp.maximum(carry[2 * h], jnp.max(s, axis=0, keepdims=True))
+            p = jnp.exp(s - top)
+            old = jnp.exp(carry[2 * h] - top)
+            carry[2 * h + 1] = carry[2 * h + 1] * old + jnp.sum(p, axis=0, keepdims=True)
+            carry[2 * h] = top
+            rows = slice(h * HD, (h + 1) * HD)
+            acc_ref[rows, :] = acc_ref[rows, :] * old + mix(h, j, p)
+        return tuple(carry)
+
+    last = lax.fori_loop(0, position, step, tuple(first))
+    for h in range(width // HD):
+        rows = slice(h * HD, (h + 1) * HD)
+        acc_ref[rows, :] = acc_ref[rows, :] / last[2 * h + 1]
+        total_ref[h : h + 1, :] = last[2 * h] + jnp.log(last[2 * h + 1])
+    out_ref[...] = acc_ref[...].T.astype(jnp.bfloat16)
+
+
+def attend(qkv, turned_kv, block):
+    length, width = qkv.shape[0], qkv.shape[1] // 3
+    return pl.pallas_call(
+        attend_kernel,
+        grid=(length // block,),
+        in_specs=[
+            pl.BlockSpec((block, width), lambda i: (i, 0)),
+            pl.BlockSpec((length, width), lambda i: (0, 1)),
+            pl.BlockSpec((width, length), lambda i: (1, 0)),
+        ],
+        out_specs=[
+            pl.BlockSpec((block, width), lambda i: (i, 0)),
+            pl.BlockSpec((width // HD, block), lambda i: (0, i)),
+        ],
+        out_shape=[
+            jax.ShapeDtypeStruct((length, width), jnp.bfloat16),
+            jax.ShapeDtypeStruct((width // HD, length), jnp.float32),
+        ],
+        scratch_shapes=[pltpu.VMEM((width, block), jnp.float32)],
+        name="attend",
+    )(qkv, qkv, turned_kv)
+
+
+def attend_back_kernel(
+    q_ref, k_ref, v_ref, kt_ref, grad_ref, out_ref, total_ref, back_ref, dq_ref, dk_ref, dv_ref
+):
+    block, width = q_ref.shape
+    position = pl.program_id(0)
     score_scale = 1.0 / math.sqrt(HD)
-    query_heads = queries.reshape(length, groups, HD)
-    key_heads = key_rows.reshape(length, groups, HD)
-    value_heads = value_rows.reshape(length, groups, HD)
-    out_blocks = []
-    totals = []
-    for position in range(length // block_rows):
-        first_row = position * block_rows
-        last_row = first_row + block_rows
-        scores = masked_scores(
-            query_heads[first_row:last_row], key_heads[:last_row], first_row, score_scale
-        )
-        row_max = jnp.max(scores, axis=-1, keepdims=True)
-        exp_scores = jnp.exp(scores - row_max)
-        row_total = jnp.sum(exp_scores, axis=-1, keepdims=True)
-        weights = (exp_scores / row_total).astype(jnp.bfloat16)
-        out_blocks.append(
-            jnp.einsum(
-                "gqk,kgd->qgd", weights, value_heads[:last_row], preferred_element_type=jnp.float32
+
+    @pl.when(position == 0)
+    def _():
+        dk_ref[...] = jnp.zeros_like(dk_ref)
+        dv_ref[...] = jnp.zeros_like(dv_ref)
+
+    dq_ref[...] = jnp.zeros_like(dq_ref)
+    scaled = q_ref[...] * jnp.asarray(score_scale, jnp.bfloat16)
+    grads = grad_ref[...]
+    zero = jnp.zeros_like(scaled)
+    query_heads = [
+        jnp.where(head_lanes((block, width), h), scaled, zero) for h in range(width // HD)
+    ]
+    grad_heads = [
+        jnp.where(head_lanes((block, width), h), grads, zero) for h in range(width // HD)
+    ]
+    shared = (grads.astype(jnp.float32) * out_ref[...].astype(jnp.float32)).T
+    inner = [
+        jnp.sum(shared[h * HD : (h + 1) * HD, :], axis=0, keepdims=True)
+        for h in range(width // HD)
+    ]
+
+    def chunk(j, masked):
+        rows = pl.ds(pl.multiple_of(j * block, block), block)
+        keys = k_ref[rows, :]
+        values = v_ref[rows, :]
+        dk = dk_ref[rows, :]
+        dv = dv_ref[rows, :]
+        for h in range(width // HD):
+            s = lax.dot_general(keys, query_heads[h], NT, preferred_element_type=jnp.float32)
+            p = jnp.exp(s - total_ref[h : h + 1, :])
+            if masked:
+                p = jnp.where(causal((block, block)), p, 0.0)
+            dp = lax.dot_general(values, grad_heads[h], NT, preferred_element_type=jnp.float32)
+            ds = (p * (dp - inner[h])).astype(jnp.bfloat16)
+            dv += jnp.dot(
+                p.astype(jnp.bfloat16), grad_heads[h], preferred_element_type=jnp.float32
             )
-        )
-        totals.append(row_max + jnp.log(row_total))
-    return (jnp.concatenate(out_blocks, axis=0).reshape(length, width), totals)
-
-
-def attend_back(queries, key_rows, value_rows, grad_rows, totals, block_rows, first):
-    length, width = queries.shape
-    groups = width // HD
-    score_scale = 1.0 / math.sqrt(HD)
-    query_heads = queries.reshape(length, groups, HD)
-    key_heads = key_rows.reshape(length, groups, HD)
-    value_heads = value_rows.reshape(length, groups, HD)
-    grad_heads = grad_rows.reshape(length, groups, HD)
-    grad_keys = jnp.zeros((length, groups, HD), jnp.float32)
-    grad_values = jnp.zeros((length, groups, HD), jnp.float32)
-    query_parts = []
-    for position in range(length // block_rows):
-        first_row = position * block_rows
-        last_row = first_row + block_rows
-        rows_q = query_heads[first_row:last_row]
-        if last_row == length:
-            rows_q, grad_rows = lax.optimization_barrier(((rows_q, grad_heads), first))[0]
-            grad_heads = grad_rows
-        scores = masked_scores(rows_q, key_heads[:last_row], first_row, score_scale)
-        weights = jnp.exp(scores - totals[position])
-        rounded = weights.astype(jnp.bfloat16)
-        grad_block = grad_heads[first_row:last_row]
-        grad_values = grad_values.at[:last_row].add(
-            jnp.einsum("gqk,qgd->kgd", rounded, grad_block, preferred_element_type=jnp.float32)
-        )
-        grad_weights = jnp.einsum(
-            "qgd,kgd->gqk", grad_block, value_heads[:last_row], preferred_element_type=jnp.float32
-        )
-        inner_sum = jnp.sum(weights * grad_weights, axis=-1, keepdims=True)
-        grad_scores = (weights * (grad_weights - inner_sum)).astype(jnp.bfloat16)
-        query_parts.append(
-            jnp.einsum(
-                "gqk,kgd->qgd",
-                grad_scores,
-                key_heads[:last_row],
-                preferred_element_type=jnp.float32,
+            dk += jnp.dot(ds, query_heads[h], preferred_element_type=jnp.float32)
+            lanes = slice(h * HD, (h + 1) * HD)
+            dq_ref[lanes, :] += jnp.dot(
+                kt_ref[lanes, rows], ds, preferred_element_type=jnp.float32
             )
-            * score_scale
-        )
-        grad_keys = grad_keys.at[:last_row].add(
-            jnp.einsum("gqk,qgd->kgd", grad_scores, rows_q, preferred_element_type=jnp.float32)
-            * score_scale
-        )
-    grad_queries = jnp.concatenate(query_parts, axis=0).reshape(length, width).astype(jnp.bfloat16)
-    return (
-        grad_queries,
-        grad_keys.reshape(length, width).astype(jnp.bfloat16),
-        grad_values.reshape(length, width).astype(jnp.bfloat16),
-    )
+        dk_ref[rows, :] = dk
+        dv_ref[rows, :] = dv
+
+    def step(j, carry):
+        chunk(j, False)
+        return carry
+
+    lax.fori_loop(0, position, step, 0)
+    chunk(position, True)
+    rows = pl.ds(pl.multiple_of(position * block, block), block)
+    back_ref[rows, :width] = (dq_ref[...] * score_scale).T.astype(jnp.bfloat16)
+
+    @pl.when(position == pl.num_programs(0) - 1)
+    def _():
+        back_ref[:, width : 2 * width] = dk_ref[...].astype(jnp.bfloat16)
+        back_ref[:, 2 * width :] = dv_ref[...].astype(jnp.bfloat16)
+
+
+def attend_back(qkv, turned_kv, grad_rows, attended, totals, block):
+    length, width = grad_rows.shape
+    return pl.pallas_call(
+        attend_back_kernel,
+        grid=(length // block,),
+        in_specs=[
+            pl.BlockSpec((block, width), lambda i: (i, 0)),
+            pl.BlockSpec((length, width), lambda i: (0, 1)),
+            pl.BlockSpec((length, width), lambda i: (0, 2)),
+            pl.BlockSpec((width, length), lambda i: (0, 0)),
+            pl.BlockSpec((block, width), lambda i: (i, 0)),
+            pl.BlockSpec((block, width), lambda i: (i, 0)),
+            pl.BlockSpec((width // HD, block), lambda i: (0, i)),
+        ],
+        out_specs=pl.BlockSpec((length, 3 * width), lambda i: (0, 0)),
+        out_shape=jax.ShapeDtypeStruct((length, 3 * width), jnp.bfloat16),
+        scratch_shapes=[
+            pltpu.VMEM((width, block), jnp.float32),
+            pltpu.VMEM((length, width), jnp.float32),
+            pltpu.VMEM((length, width), jnp.float32),
+        ],
+        name="attend_back",
+    )(qkv, qkv, qkv, turned_kv, grad_rows, attended, totals)
 
 
 def contract_rows(left_op, right_op):
@@ -255,7 +344,8 @@
     last_in = send(last.astype(bf16), inward)
     following = block(2)
     following_in = send(following.astype(bf16), inward)
-    away_in = send(block(1 - inner).astype(bf16), near_moves)
+    away = block(1 - inner).astype(bf16)
+    away_in = send(away, near_moves)
     mine = block(inner)
     last = (last + last_in.astype(jnp.float32)).astype(bf16)
     last = send(last, both([(1, 3), (2, 0)]))
@@ -271,7 +361,9 @@
     far = jnp.where(inner, following, last).astype(jnp.float32)
     keeps = lax.axis_index("pair") == place // 2
     kept = jnp.where(keeps, mine, far)
-    given = swap(jnp.where(keeps, far, mine).astype(jnp.bfloat16)).astype(jnp.float32)
+    given = jnp.where(keeps, far, mine).astype(jnp.bfloat16)
+    given = swap(given)
+    given = given.astype(jnp.float32)
     return in_order(kept, given, 1)
 
 
@@ -370,9 +462,9 @@
     qkv = jnp.dot(seq_a, w_cols, preferred_element_type=f32).astype(bf16)
     down_parts = jnp.concatenate(down_parts, axis=1)
     full_down = lax.all_gather(down_parts, "outer", axis=0, tiled=True)
-    queries, key_rows, value_rows = (qkv[:, i * width : (i + 1) * width] for i in range(3))
-    attended, totals = attend(queries, key_rows, value_rows, block_rows)
-    attended = group_to_rows(attended.astype(bf16))
+    turned_kv = qkv[:, width:].T
+    seen, totals = attend(qkv, turned_kv, block_rows)
+    attended = group_to_rows(seen)
     out_other = swap(out_own)
     place = lax.axis_index("pair")
     full_o = jnp.stack(
@@ -417,13 +509,9 @@
     grad_att = after(grad_att, (grad_down, grad_up, grad_o))
     grad_down = lax.psum_scatter(grad_down, "outer", scatter_dimension=0, tiled=True)
     grad_up = lax.psum_scatter(grad_up, "outer", scatter_dimension=0, tiled=True)
-    grad_queries, grad_keys, grad_values = attend_back(
-        queries, key_rows, value_rows, grad_att, totals, block_rows, (grad_down, grad_up)
-    )
+    grad_qkv = attend_back(qkv, turned_kv, grad_att, seen, totals, block_rows)
     grad_down = scatter_half(grad_down).T
     grad_up = scatter_half(grad_up)
-    grad_qkv = jnp.concatenate([grad_queries, grad_keys, grad_values], axis=1)
-    grad_qkv = after(grad_qkv, (grad_down, grad_up))
     grad_a = contract_cols(grad_qkv, w_cols).astype(bf16)
     grad_w = contract_rows(seq_a, after(grad_qkv, grad_a)).astype(bf16)
     grad_a = sequence_sum(grad_a)

time: 591 us -> 584 us (0.988)
  matrix products: 159 us -> 79.1 us
  Pallas kernels: 0 us -> 59.8 us
  waiting for transfers between devices: 164 us -> 201 us
  other arithmetic: 93.2 us -> 56.4 us
  starting transfers between devices: 101 us -> 120 us
  local copies, waits for them, and re-layouts: 50.5 us -> 43.2 us
    dot_general x25 -> x0, matrix products: 89.4 us -> none  [the longest x4 31.5 us: attend_back(): jnp.einsum('qgd,kgd->gqk', grad_block, value_heads[:last_row], preferred_...]
    pallas_call x0 -> x2, Pallas kernels: none -> 59.8 us  [the longest x1 34.3 us: attend_back(): pl.pallas_call(attend_back_kernel, grid=(length // block,), in_specs=[pl....]
    reduce_scatter x1, waiting for transfers between devices: 0.01 us -> 42.8 us  [layer(): lax.psum_scatter(grad_down, 'outer', scatter_dimension=0, tiled=True)]
    ppermute x26, waiting for transfers between devices: 93.1 us -> 66.9 us  [send(): lax.ppermute(values, LINE, [(a * HEADS + b, c * HEADS + d) for (a, b), (c...]
    ppermute x15, starting transfers between devices: 8.97 us -> 30.7 us  [swap(): return lax.ppermute(values, 'pair', [(0, 1), (1, 0)])]
    convert_element_type x7 -> x3, other arithmetic: 23.2 us -> 2.61 us  [the longest x1 1.56 us: sequence_end(): given = jnp.where(keeps, far, mine).astype(jnp.bfloat16)]
    ppermute x18, waiting for transfers between devices: 58.3 us -> 74.1 us  [shift(): lax.ppermute(values, 'head', [(i, (i + step) % HEADS) for i in range(HEAD...]
    reduce_sum x4 -> x0, other arithmetic: 8.88 us -> none  [attend(): row_total = jnp.sum(exp_scores, axis=-1, keepdims=True)]
  transfers between devices with their start and end apart: 70 -> 70, of which waited for: 28 -> 30; matrix products, arithmetic and copies ran while one was open for 43% -> 20% of each run, Pallas kernels for 0% -> 10%
where the time goes in v1:
time: 584 us; the launch traced here: 575 us
  waiting for transfers between devices  201 us (34%)
  starting transfers between devices  120 us (21%)
  matrix products  79.1 us (14%)
  Pallas kernels  59.8 us (10%)
  other arithmetic  56.4 us (10%)
  local copies, waits for them, and re-layouts  43.2 us (7%)
  between operations  15.5 us (3%)
    ppermute x18, waiting for transfers between devices, shift(): lax.ppermute(values, 'head', [(i, (i + step) % HEADS) for i in range(HEAD...  74.1 us
    ppermute x26, waiting for transfers between devices, send(): lax.ppermute(values, LINE, [(a * HEADS + b, c * HEADS + d) for (a, b), (c...  66.9 us
    ppermute x26, starting transfers between devices, send(): lax.ppermute(values, LINE, [(a * HEADS + b, c * HEADS + d) for (a, b), (c...  59.6 us
    reduce_scatter x1, waiting for transfers between devices, layer(): lax.psum_scatter(grad_down, 'outer', scatter_dimension=0, tiled=True)  42.8 us
    pallas_call x1, Pallas kernels, attend_back(): pl.pallas_call(attend_back_kernel, grid=(length // block,), in_specs=[pl....  34.3 us
    ppermute x15, starting transfers between devices, swap(): return lax.ppermute(values, 'pair', [(0, 1), (1, 0)])  30.7 us
    dot_general x4, matrix products, contract_rows(): lax.dot_general(left_op, right_op, (((0,), (0,)), ((), ())), preferred_el...  26.4 us
    pallas_call x1, Pallas kernels, attend(): pl.pallas_call(attend_kernel, grid=(length // block,), in_specs=[pl.Block...  25.5 us
  transfers between devices with their start and end apart: 70, of which 30 were waited for; matrix products, arithmetic and copies ran while one was open for 20% of the time, Pallas kernels for 10%

profile of v1, /device:TPU:0, one launch (start us, length us, event | category | flops | bytes accessed | tf_op | source)
XLA Modules:
  0.0 574.8 jit_solution(10029075468354998732)
XLA Ops:
  20.5 8.8 %collective-permute-done.12 = bf16[128,256]{1,0:T(8,128)(2,1)S(1)} collective-permute-done((bf16[128,256]{1,0:T(8,128)(2,1)S(1)}, bf16[128,256]{1,0:T(8,128)(2,1)S(1)}, u32[]{:S(2)}, u32[]{:S(2)}) %collective-permute-start.12) | collective-permute-done | bytes 65568 | tf_op jit(solution)/shard_map/ppermute | solution.py:243
  35.1 6.3 %collective-permute-done.23 = bf16[256,512]{0,1:T(8,128)(2,1)S(1)} collective-permute-done((bf16[256,512]{0,1:T(8,128)(2,1)S(1)}, bf16[256,512]{0,1:T(8,128)(2,1)S(1)}, u32[]{:S(2)}, u32[]{:S(2)}) %collective-permute-start.23) | collective-permute-done | bytes 262176 | tf_op jit(solution)/shard_map/ppermute | solution.py:243
  41.4 15.3 %collective-permute-done.22 = bf16[256,512]{0,1:T(8,128)(2,1)S(1)} collective-permute-done((bf16[256,512]{0,1:T(8,128)(2,1)S(1)}, bf16[256,512]{0,1:T(8,128)(2,1)S(1)}, u32[]{:S(2)}, u32[]{:S(2)}) %collective-permute-start.22) | collective-permute-done | bytes 262176 | tf_op jit(solution)/shard_map/ppermute | solution.py:243
  70.0 21.6 %collective-permute-start.24 = (bf16[128,512]{0,1:T(8,128)(2,1)}, bf16[128,512]{0,1:T(8,128)(2,1)S(1)}, u32[]{:S(2)}, u32[]{:S(2)}) collective-permute-start(bf16[128,512]{0,1:T(8,128)(2,1)} %get-tuple-element.156), channel_id=1, source_target_pairs={{0,4},{4,0},{1,5},{5,1},{2,6},{6,2},{3,7},{7,3},{8,12},{12,8},{9,1... | collective-permute-start | bytes 393224 | tf_op jit(solution)/shard_map/ppermute | solution.py:231
  99.4 6.0 %collective-permute-done.4 = bf16[512,1024]{1,0:T(8,128)(2,1)} collective-permute-done((bf16[512,1024]{1,0:T(8,128)(2,1)S(1)}, bf16[512,1024]{1,0:T(8,128)(2,1)}, u32[]{:S(2)}, u32[]{:S(2)}) %collective-permute-start.4) | collective-permute-done | bytes 1048608 | tf_op jit(solution)/shard_map/ppermute | solution.py:235
  109.1 13.1 %collective-permute-done.27 = bf16[256,512]{0,1:T(8,128)(2,1)S(1)} collective-permute-done((bf16[256,512]{0,1:T(8,128)(2,1)S(1)}, bf16[256,512]{0,1:T(8,128)(2,1)S(1)}, u32[]{:S(2)}, u32[]{:S(2)}) %collective-permute-start.27) | collective-permute-done | bytes 262176 | tf_op jit(solution)/shard_map/ppermute | solution.py:243
  123.7 13.2 %collective-permute-done.26 = bf16[256,512]{0,1:T(8,128)(2,1)S(1)} collective-permute-done((bf16[256,512]{0,1:T(8,128)(2,1)S(1)}, bf16[256,512]{0,1:T(8,128)(2,1)S(1)}, u32[]{:S(2)}, u32[]{:S(2)}) %collective-permute-start.26) | collective-permute-done | bytes 262176 | tf_op jit(solution)/shard_map/ppermute | solution.py:243
  165.0 25.5 %attend.1 = (bf16[2048,256]{1,0:T(8,128)(2,1)}, f32[4,2048]{1,0:T(4,128)}) custom-call(bf16[2048,768]{1,0:T(8,128)(2,1)} %copy.77.q_ref.k_ref.v_ref, bf16[2048,768]{1,0:T(8,128)(2,1)} %copy.77.q_ref.k_ref.v_ref, bf16[512,2048]{1,0:T(8,128)(2,1)} %slice_bitcast_fusion.vt_ref.kt_ref), custom_call_target="tpu_custom_call" | custom-call | tf_op jit(solution)/shard_map/attend/pallas_call | solution.py:99
  197.3 6.0 %collective-permute-start.17 = (bf16[512,256]{1,0:T(8,128)(2,1)S(1)}, bf16[512,256]{1,0:T(8,128)(2,1)S(1)}, u32[]{:S(2)}, u32[]{:S(2)}) collective-permute-start(bf16[512,256]{1,0:T(8,128)(2,1)S(1)} %get-tuple-element.137), channel_id=1, source_target_pairs={{0,3},{1,1},{2,7},{3,5},{4,0},{5,2},{6,4},{7,6},{8,11},{9,9},{10,1... | collective-permute-start | bytes 786440 | tf_op jit(solution)/shard_map/ppermute | solution.py:235
  225.1 10.7 %fusion.32 = f32[1024,2048]{1,0:T(8,128)} fusion(bf16[1024,2048]{0,1:T(8,128)(2,1)} %all-gather.6.cloned.1.call-done, bf16[512,1024]{1,0:T(8,128)(2,1)} %collective-permute-done.19, bf16[512,1024]{1,0:T(8,128)(2,1)} %copy-done.22), kind=kOutput, calls=%fused_computation.77 | convolution fusion | flops 4299161600 | bytes 14680064 | tf_op jit(solution)/shard_map/dot_general | solution.py:480
  235.8 9.0 %fusion.45 = f32[1024,1024]{1,0:T(8,128)S(1)} fusion(bf16[1024,2048]{0,1:T(8,128)(2,1)} %all-gather.8.cloned.1.call-done, f32[1024,2048]{1,0:T(8,128)} %fusion.32), kind=kOutput, calls=%fused_computation.177 | convolution fusion | flops 4313841664 | bytes 16777216 | tf_op jit(solution)/shard_map/dot_general | solution.py:219
  256.0 12.8 %fusion.6 = bf16[1024,2048]{1,0:T(8,128)(2,1)S(1)} fusion(f32[1024,2048]{1,0:T(8,128)} %fusion.32, bf16[1024,2048]{0,1:T(8,128)(2,1)} %all-gather.8.cloned.1.call-done, bf16[512,1024]{1,0:T(8,128)(2,1)} %collective-permute-done.29, bf16[512,1024]{1,0:T(8,128)(2,1)} %get-tuple-element.113), kind=kOutput, calls=%fused_computation.8 | convolution fusion | flops 4341104640 | bytes 18874368 | tf_op jit(solution)/shard_map/dot_general | solution.py:492
  276.8 10.9 %convolution_convert_fusion.2 = bf16[1024,2048]{1,0:T(8,128)(2,1)} fusion(bf16[512,1024]{1,0:T(8,128)(2,1)} %collective-permute-done.29, bf16[512,1024]{1,0:T(8,128)(2,1)} %get-tuple-element.113, f32[1024,2048]{1,0:T(8,128)} %fusion.32), kind=kOutput, calls=%fused_computation.13 | convolution fusion | flops 4320133120 | bytes 14680064 | tf_op jit(solution)/shard_map/dot_general | solution.py:213
  287.6 9.6 %convolution_convert_fusion.1 = bf16[1024,2048]{1,0:T(8,128)(2,1)} fusion(bf16[1024,2048]{1,0:T(8,128)(2,1)} %copy-done.51, bf16[512,1024]{1,0:T(8,128)(2,1)} %collective-permute-done.19, bf16[512,1024]{1,0:T(8,128)(2,1)} %copy-done.22), kind=kOutput, calls=%fused_computation.12 | convolution fusion | flops 4301258752 | bytes 10485760 | tf_op jit(solution)/shard_map/dot_general | solution.py:213
  321.6 10.4 %collective-permute-done.32 = bf16[512,256]{1,0:T(8,128)(2,1)S(1)} collective-permute-done((bf16[512,256]{1,0:T(8,128)(2,1)S(1)}, bf16[512,256]{1,0:T(8,128)(2,1)S(1)}, u32[]{:S(2)}, u32[]{:S(2)}) %collective-permute-start.32) | collective-permute-done | bytes 262176 | tf_op jit(solution)/shard_map/ppermute | solution.py:235
  333.3 34.3 %attend_back.1 = bf16[2048,768]{1,0:T(8,128)(2,1)} custom-call(bf16[2048,768]{1,0:T(8,128)(2,1)} %copy.77.q_ref.k_ref.v_ref, bf16[2048,768]{1,0:T(8,128)(2,1)} %copy.77.q_ref.k_ref.v_ref, bf16[2048,768]{1,0:T(8,128)(2,1)} %copy.77.q_ref.k_ref.v_ref, bf16[512,2048]{1,0:T(8,128)(2,1)} %slice_bitcast_fusion.vt_ref.kt_ref, ...), custom_call_target="tpu_custom_call" | custom-call | tf_op jit(solution)/shard_map/attend_back/pallas_call | solution.py:189
  367.6 8.0 %convolution_convert_fusion = bf16[2048,1024]{1,0:T(8,128)(2,1)} fusion(bf16[2048,768]{1,0:T(8,128)(2,1)} %attend_back.1, bf16[1024,1280]{1,0:T(8,128)(2,1)} %all-gather.4.cloned.1.call-done), kind=kOutput, calls=%fused_computation.11 | convolution fusion | flops 3223322624 | bytes 8912896 | tf_op jit(solution)/shard_map/dot_general | solution.py:219
  395.0 8.1 %collective-permute-start.39 = (bf16[512,512]{1,0:T(8,128)(2,1)S(1)}, bf16[512,512]{1,0:T(8,128)(2,1)S(1)}, u32[]{:S(2)}, u32[]{:S(2)}) collective-permute-start(bf16[512,512]{1,0:T(8,128)(2,1)S(1)} %fusion.34), channel_id=1, source_target_pairs={{0,1},{3,2},{4,5},{7,6},{8,9},{11,10},{12,13},{15,14},{16,17},{19,... | collective-permute-start | bytes 1572872 | tf_op jit(solution)/shard_map/ppermute | solution.py:235
  405.2 10.2 %collective-permute-done.39 = bf16[512,512]{1,0:T(8,128)(2,1)S(1)} collective-permute-done((bf16[512,512]{1,0:T(8,128)(2,1)S(1)}, bf16[512,512]{1,0:T(8,128)(2,1)S(1)}, u32[]{:S(2)}, u32[]{:S(2)}) %collective-permute-start.39) | collective-permute-done | bytes 524320 | tf_op jit(solution)/shard_map/ppermute | solution.py:235
  417.1 8.7 %collective-permute-done.42 = bf16[512,512]{1,0:T(8,128)(2,1)S(1)} collective-permute-done((bf16[512,512]{1,0:T(8,128)(2,1)S(1)}, bf16[512,512]{1,0:T(8,128)(2,1)S(1)}, u32[]{:S(2)}, u32[]{:S(2)}) %collective-permute-start.42) | collective-permute-done | bytes 524320 | tf_op jit(solution)/shard_map/ppermute | solution.py:235
  432.3 11.8 %collective-permute-done.43 = bf16[512,512]{1,0:T(8,128)(2,1)} collective-permute-done((bf16[512,512]{1,0:T(8,128)(2,1)}, bf16[512,512]{1,0:T(8,128)(2,1)}, u32[]{:S(2)}, u32[]{:S(2)}) %collective-permute-start.43) | collective-permute-done | bytes 524320 | tf_op jit(solution)/shard_map/ppermute | solution.py:235
  444.1 10.6 %collective-permute-done.37 = bf16[512,512]{1,0:T(8,128)(2,1)} collective-permute-done((bf16[512,512]{1,0:T(8,128)(2,1)}, bf16[512,512]{1,0:T(8,128)(2,1)}, u32[]{:S(2)}, u32[]{:S(2)}) %collective-permute-start.37) | collective-permute-done | bytes 524320 | tf_op jit(solution)/shard_map/ppermute | solution.py:235
  498.1 42.8 %reduce-scatter.8.cloned.1.call-done = bf16[256,2048]{1,0:T(8,128)(2,1)} async-done(((bf16[1024,2048]{1,0:T(8,128)(2,1)}), bf16[256,2048]{1,0:T(8,128)(2,1)}) %reduce-scatter.8.cloned.1.call-update) | async-done | bytes 1048592 | tf_op jit(solution)/shard_map/reduce_scatter | solution.py:510
  553.2 10.0 %collective-permute-done.56 = bf16[256,512]{1,0:T(8,128)(2,1)S(1)} collective-permute-done((bf16[256,512]{1,0:T(8,128)(2,1)S(1)}, bf16[256,512]{1,0:T(8,128)(2,1)S(1)}, u32[]{:S(2)}, u32[]{:S(2)}) %collective-permute-start.56) | collective-permute-done | bytes 262176 | tf_op jit(solution)/shard_map/ppermute | solution.py:243
  (350 shorter events, 235.3 us)
Async XLA Ops:
  7.2 140.8 %all-gather.4.cloned.1.call-start = ((), (), s32[]{:S(2)}) async-start(), calls=%async_computation.3 | async-start | bytes 3276800 | tf_op jit(solution)/shard_map/all_gather | solution.py:449
  30.2 194.8 %all-gather.6.cloned.1.call-start = ((), (), s32[]{:S(2)}) async-start(), calls=%async_computation.4 | async-start | bytes 5242880 | tf_op jit(solution)/shard_map/all_gather | solution.py:457
  33.3 23.5 %collective-permute-start.22 = (bf16[256,512]{0,1:T(8,128)(2,1)S(1)}, bf16[256,512]{0,1:T(8,128)(2,1)S(1)}, u32[]{:S(2)}, u32[]{:S(2)}) collective-permute-start(bf16[256,512]{0,1:T(8,128)(2,1)S(1)} %maximum_select_fusion.2), channel_id=1, source_target_pairs={{0,2},{1,3},{2,0},{3,1},{4,6},{5,7},{6,4},{7,5},{8,10},{9,11},{10,... | collective-permute-start | bytes 786440 | tf_op jit(solution)/shard_map/ppermute | solution.py:243
  33.3 23.4 %collective-permute-start.21 = (bf16[256,512]{0,1:T(8,128)(2,1)S(1)}, bf16[256,512]{0,1:T(8,128)(2,1)S(1)}, u32[]{:S(2)}, u32[]{:S(2)}) collective-permute-start(bf16[256,512]{0,1:T(8,128)(2,1)S(1)} %maximum_select_fusion.2), channel_id=1, source_target_pairs={{0,1},{1,2},{2,3},{3,0},{4,5},{5,6},{6,7},{7,4},{8,9},{9,10},{10,1... | collective-permute-start | bytes 786440 | tf_op jit(solution)/shard_map/ppermute | solution.py:243
  57.9 177.9 %all-gather.8.cloned.1.call-start = ((), (), s32[]{:S(2)}) async-start(), calls=%async_computation.5 | async-start | bytes 5242880 | tf_op jit(solution)/shard_map/all_gather | solution.py:464
  62.7 33.7 %collective-permute-start.1 = (bf16[512,1024]{1,0:T(8,128)(2,1)}, bf16[512,1024]{1,0:T(8,128)(2,1)}, u32[]{:S(2)}, u32[]{:S(2)}) collective-permute-start(bf16[512,1024]{1,0:T(8,128)(2,1)} %fusion.17), channel_id=1, source_target_pairs={{0,1},{1,0},{6,7},{7,6},{8,9},{9,8},{14,15},{15,14},{16,17},{17,16... | collective-permute-start | bytes 3145736 | tf_op jit(solution)/shard_map/ppermute | solution.py:235
  66.7 38.8 %collective-permute-start.4 = (bf16[512,1024]{1,0:T(8,128)(2,1)S(1)}, bf16[512,1024]{1,0:T(8,128)(2,1)}, u32[]{:S(2)}, u32[]{:S(2)}) collective-permute-start(bf16[512,1024]{1,0:T(8,128)(2,1)S(1)} %collective-permute-done.3), channel_id=1, source_target_pairs={{1,0},{6,7},{9,8},{14,15},{17,16},{22,23},{25,24},{30,31}} | collective-permute-start | bytes 3145736 | tf_op jit(solution)/shard_map/ppermute | solution.py:235
  68.1 54.2 %collective-permute-start.7 = (bf16[512,1024]{1,0:T(8,128)(2,1)S(1)}, bf16[512,1024]{1,0:T(8,128)(2,1)}, u32[]{:S(2)}, u32[]{:S(2)}) collective-permute-start(bf16[512,1024]{1,0:T(8,128)(2,1)S(1)} %collective-permute-done.6), channel_id=1, source_target_pairs={{1,0},{6,7},{9,8},{14,15},{17,16},{22,23},{25,24},{30,31}} | collective-permute-start | bytes 3145736 | tf_op jit(solution)/shard_map/ppermute | solution.py:235
  70.0 24.5 %collective-permute-start.24 = (bf16[128,512]{0,1:T(8,128)(2,1)}, bf16[128,512]{0,1:T(8,128)(2,1)S(1)}, u32[]{:S(2)}, u32[]{:S(2)}) collective-permute-start(bf16[128,512]{0,1:T(8,128)(2,1)} %get-tuple-element.156), channel_id=1, source_target_pairs={{0,4},{4,0},{1,5},{5,1},{2,6},{6,2},{3,7},{7,3},{8,12},{12,8},{9,1... | collective-permute-start | bytes 393224 | tf_op jit(solution)/shard_map/ppermute | solution.py:231
  91.7 50.7 %collective-permute-start = (bf16[512,1024]{1,0:T(8,128)(2,1)}, bf16[512,1024]{1,0:T(8,128)(2,1)}, u32[]{:S(2)}, u32[]{:S(2)}) collective-permute-start(bf16[512,1024]{1,0:T(8,128)(2,1)} %fusion.17), channel_id=1, source_target_pairs={{0,4},{1,5},{6,2},{7,3},{8,12},{9,13},{14,10},{15,11},{16,20},{17,... | collective-permute-start | bytes 3145736 | tf_op jit(solution)/shard_map/ppermute | solution.py:235
  96.3 25.9 %collective-permute-start.27 = (bf16[256,512]{0,1:T(8,128)(2,1)S(1)}, bf16[256,512]{0,1:T(8,128)(2,1)S(1)}, u32[]{:S(2)}, u32[]{:S(2)}) collective-permute-start(bf16[256,512]{0,1:T(8,128)(2,1)S(1)} %maximum_select_fusion.3), channel_id=1, source_target_pairs={{0,3},{1,0},{2,1},{3,2},{4,7},{5,4},{6,5},{7,6},{8,11},{9,8},{10,9... | collective-permute-start | bytes 786440 | tf_op jit(solution)/shard_map/ppermute | solution.py:243
  96.4 46.0 %collective-permute-start.2 = (bf16[512,1024]{1,0:T(8,128)(2,1)}, bf16[512,1024]{1,0:T(8,128)(2,1)}, u32[]{:S(2)}, u32[]{:S(2)}) collective-permute-start(bf16[512,1024]{1,0:T(8,128)(2,1)} %collective-permute-done.1), channel_id=1, source_target_pairs={{0,4},{1,5},{6,2},{7,3},{8,12},{9,13},{14,10},{15,11},{16,20},{17,... | collective-permute-start | bytes 3145736 | tf_op jit(solution)/shard_map/ppermute | solution.py:235
  106.8 35.6 %collective-permute-start.5 = (bf16[512,1024]{1,0:T(8,128)(2,1)S(1)}, bf16[512,1024]{1,0:T(8,128)(2,1)}, u32[]{:S(2)}, u32[]{:S(2)}) collective-permute-start(bf16[512,1024]{1,0:T(8,128)(2,1)S(1)} %broadcast_select_fusion.1), channel_id=1, source_target_pairs={{0,4},{1,5},{6,2},{7,3},{8,12},{9,13},{14,10},{15,11},{16,20},{17,... | collective-permute-start | bytes 3145736 | tf_op jit(solution)/shard_map/ppermute | solution.py:235
  142.0 302.1 %reduce-scatter.4.cloned.1.call-start = ((), (), s32[]{:S(2)}) async-start(), calls=%async_computation.6 | async-start | bytes 3276800 | tf_op jit(solution)/shard_map/reduce_scatter | solution.py:521
  150.5 61.3 %collective-permute-start.18 = (bf16[4,128,1024]{2,1,0:T(8,128)(2,1)}, bf16[4,128,1024]{2,1,0:T(8,128)(2,1)S(1)}, u32[]{:S(2)}, u32[]{:S(2)}) collective-permute-start(bf16[4,128,1024]{2,1,0:T(8,128)(2,1)} %pad_maximum_fusion.11), channel_id=1, source_target_pairs={{0,4},{4,0},{1,5},{5,1},{2,6},{6,2},{3,7},{7,3},{8,12},{12,8},{9,1... | collective-permute-start | bytes 3145736 | tf_op jit(solution)/shard_map/ppermute | solution.py:231
  320.1 60.1 %collective-permute-start.44 = (bf16[4,1,128,1024]{3,2,1,0:T(8,128)(2,1)}, bf16[4,1,128,1024]{3,2,1,0:T(8,128)(2,1)}, u32[]{:S(2)}, u32[]{:S(2)}) collective-permute-start(bf16[4,1,128,1024]{3,2,1,0:T(8,128)(2,1)} %constant_dynamic-slice_fusion.6), channel_id=1, source_target_pairs={{0,4},{4,0},{1,5},{5,1},{2,6},{6,2},{3,7},{7,3},{8,12},{12,8},{9,1... | collective-permute-start | bytes 3145736 | tf_op jit(solution)/shard_map/ppermute | solution.py:231
  385.7 103.0 %reduce-scatter.6.cloned.1.call-start = ((), (), s32[]{:S(2)}) async-start(), calls=%async_computation.7 | async-start | bytes 5242880 | tf_op jit(solution)/shard_map/reduce_scatter | solution.py:511
  386.3 154.6 %reduce-scatter.8.cloned.1.call-start = ((), (), s32[]{:S(2)}) async-start(), calls=%async_computation.8 | async-start | bytes 5242880 | tf_op jit(solution)/shard_map/reduce_scatter | solution.py:510
  404.6 23.5 %collective-permute-start.36 = (bf16[512,512]{1,0:T(8,128)(2,1)S(1)}, bf16[512,512]{1,0:T(8,128)(2,1)S(1)}, u32[]{:S(2)}, u32[]{:S(2)}) collective-permute-start(bf16[512,512]{1,0:T(8,128)(2,1)S(1)} %get-tuple-element.30), channel_id=1, source_target_pairs={{0,4},{4,0},{1,5},{5,1},{2,6},{6,2},{3,7},{7,3},{8,12},{12,8},{9,1... | collective-permute-start | bytes 1572872 | tf_op jit(solution)/shard_map/ppermute | solution.py:231
  404.7 39.4 %collective-permute-start.35 = (bf16[512,512]{1,0:T(8,128)(2,1)S(1)}, bf16[512,512]{1,0:T(8,128)(2,1)S(1)}, u32[]{:S(2)}, u32[]{:S(2)}) collective-permute-start(bf16[512,512]{1,0:T(8,128)(2,1)S(1)} %get-tuple-element.28), channel_id=1, source_target_pairs={{0,4},{4,0},{1,5},{5,1},{2,6},{6,2},{3,7},{7,3},{8,12},{12,8},{9,1... | collective-permute-start | bytes 1572872 | tf_op jit(solution)/shard_map/ppermute | solution.py:231
  429.0 25.8 %collective-permute-start.37 = (bf16[512,512]{1,0:T(8,128)(2,1)}, bf16[512,512]{1,0:T(8,128)(2,1)}, u32[]{:S(2)}, u32[]{:S(2)}) collective-permute-start(bf16[512,512]{1,0:T(8,128)(2,1)} %add_convert_fusion.5), channel_id=1, source_target_pairs={{0,1},{1,0},{2,3},{3,2},{4,5},{5,4},{6,7},{7,6},{8,9},{9,8},{10,11... | collective-permute-start | bytes 1572872 | tf_op jit(solution)/shard_map/ppermute | solution.py:235
  490.8 55.2 %collective-permute-start.53 = (bf16[256,512]{1,0:T(8,128)(2,1)}, bf16[256,512]{1,0:T(8,128)(2,1)S(1)}, u32[]{:S(2)}, u32[]{:S(2)}) collective-permute-start(bf16[256,512]{1,0:T(8,128)(2,1)} %get-tuple-element.123), channel_id=1, source_target_pairs={{0,1},{1,2},{2,3},{3,0},{4,5},{5,6},{6,7},{7,4},{8,9},{9,10},{10,1... | collective-permute-start | bytes 786440 | tf_op jit(solution)/shard_map/ppermute | solution.py:243
  492.2 55.3 %collective-permute-start.52 = (bf16[256,512]{1,0:T(8,128)(2,1)}, bf16[256,512]{1,0:T(8,128)(2,1)}, u32[]{:S(2)}, u32[]{:S(2)}) collective-permute-start(bf16[256,512]{1,0:T(8,128)(2,1)} %get-tuple-element.124), channel_id=1, source_target_pairs={{0,2},{1,3},{2,0},{3,1},{4,6},{5,7},{6,4},{7,5},{8,10},{9,11},{10,... | collective-permute-start | bytes 786440 | tf_op jit(solution)/shard_map/ppermute | solution.py:243
  493.0 54.5 %collective-permute-start.51 = (bf16[256,512]{1,0:T(8,128)(2,1)}, bf16[256,512]{1,0:T(8,128)(2,1)}, u32[]{:S(2)}, u32[]{:S(2)}) collective-permute-start(bf16[256,512]{1,0:T(8,128)(2,1)} %get-tuple-element.122), channel_id=1, source_target_pairs={{0,3},{1,0},{2,1},{3,2},{4,7},{5,4},{6,5},{7,6},{8,11},{9,8},{10,9... | collective-permute-start | bytes 786440 | tf_op jit(solution)/shard_map/ppermute | solution.py:243
  (100 other events, 904.8 us)
Sparse Core Ops, SparseCore 0:
  30.3 38.3 all-gather.3
  70.6 52.4 all-gather.5
  142.2 50.6 all-gather.7
  385.9 43.3 reduce-scatter.3
  432.1 53.2 reduce-scatter.5
  488.3 52.5 reduce-scatter.7

commit v2 on v1

--- a/solution.py
+++ b/solution.py
@@ -277,7 +277,8 @@
 
 def half_rows(block):
     own, other = halves(block, 1)
-    return in_order(own, swap(other), 0)
+    other = swap(other)
+    return in_order(own, other, 0)
 
 
 def scatter_half(rows):
@@ -325,17 +326,18 @@
     return joined
 
 
-def sequence_sum(partial):
+def sequence_sum(own_half, other_half):
     place = lax.axis_index("head")
     low = place < 2
     inner = jnp.where((place == 1) | (place == 2), 1, 0)
-    rows = partial.shape[0] // HEADS
+    rows = own_half.shape[0] // HEADS
     bf16 = jnp.bfloat16
 
     def block(i):
         index = jnp.where(low, i, HEADS - 1 - i)
-        piece = lax.dynamic_slice_in_dim(partial, index * rows, rows, 0)
-        own, other = lax.optimization_barrier(halves(piece, 1))
+        own = lax.dynamic_slice_in_dim(own_half, index * rows, rows, 0)
+        other = lax.dynamic_slice_in_dim(other_half, index * rows, rows, 0)
+        own, other = lax.optimization_barrier((own, other))
         return own.astype(jnp.float32) + swap(other).astype(jnp.float32)
 
     inward = both([(0, 1), (3, 2)])
@@ -512,9 +514,11 @@
     grad_qkv = attend_back(qkv, turned_kv, grad_att, seen, totals, block_rows)
     grad_down = scatter_half(grad_down).T
     grad_up = scatter_half(grad_up)
-    grad_a = contract_cols(grad_qkv, w_cols).astype(bf16)
-    grad_w = contract_rows(seq_a, after(grad_qkv, grad_a)).astype(bf16)
-    grad_a = sequence_sum(grad_a)
+    w_own, w_other = halves(w_cols, 0)
+    grad_a_other = contract_cols(grad_qkv, w_other).astype(bf16)
+    grad_a_own = contract_cols(grad_qkv, w_own).astype(bf16)
+    grad_w = contract_rows(seq_a, after(grad_qkv, grad_a_own)).astype(bf16)
+    grad_a = sequence_sum(grad_a_own, grad_a_other)
     grad_o = grad_o.reshape(-1, 1, w_out.shape[1], attended.shape[1])
     grad_o = jnp.concatenate(jnp.split(grad_o, 2, axis=3), axis=1).reshape(model, -1)
     grad_w = jnp.concatenate([grad_w, grad_o], axis=1)

time: 584 us -> 580 us (level)
  starting transfers between devices: 120 us -> 112 us
  waiting for transfers between devices: 201 us -> 209 us
    reduce_scatter x1, waiting for transfers between devices: 42.8 us -> 0.01 us  [layer(): lax.psum_scatter(grad_down, 'outer', scatter_dimension=0, tiled=True)]
    reduce_scatter x1, waiting for transfers between devices: 0.01 us -> 42.5 us  [layer(): lax.psum_scatter(grad_up, 'outer', scatter_dimension=0, tiled=True)]
    ppermute x26, waiting for transfers between devices: 66.9 us -> 76 us  [send(): lax.ppermute(values, LINE, [(a * HEADS + b, c * HEADS + d) for (a, b), (c...]
    dynamic_slice x2 -> x1, local copies, waits for them, and re-layouts: 7.02 us -> 1.07 us  [halves(): other = lax.dynamic_slice_in_dim(block, (1 - place) * size, size, axis)]
    unnamed x116 -> x126, local copies, waits for them, and re-layouts: 17 us -> 19.2 us
    dot_general x4 -> x5, matrix products: 22.8 us -> 23.8 us  [contract_cols(): lax.dot_general(left_op, right_op, (((1,), (1,)), ((), ())), preferred_el...]
  transfers between devices with their start and end apart: 70 -> 70, of which waited for: 30 -> 28; matrix products, arithmetic and copies ran while one was open for 20% -> 19% of each run, Pallas kernels for 10% -> 10%
where the time goes in v2:
time: 580 us; the launch traced here: 574 us
  waiting for transfers between devices  209 us (36%)
  starting transfers between devices  112 us (19%)
  matrix products  77 us (13%)
  Pallas kernels  59.9 us (10%)
  other arithmetic  56.6 us (10%)
  local copies, waits for them, and re-layouts  44.2 us (8%)
  between operations  15.8 us (3%)
    ppermute x18, waiting for transfers between devices, shift(): lax.ppermute(values, 'head', [(i, (i + step) % HEADS) for i in range(HEAD...  77.6 us
    ppermute x26, waiting for transfers between devices, send(): lax.ppermute(values, LINE, [(a * HEADS + b, c * HEADS + d) for (a, b), (c...  76 us
    ppermute x26, starting transfers between devices, send(): lax.ppermute(values, LINE, [(a * HEADS + b, c * HEADS + d) for (a, b), (c...  56.6 us
    reduce_scatter x1, waiting for transfers between devices, layer(): lax.psum_scatter(grad_up, 'outer', scatter_dimension=0, tiled=True)  42.5 us
    pallas_call x1, Pallas kernels, attend_back(): pl.pallas_call(attend_back_kernel, grid=(length // block,), in_specs=[pl....  34.4 us
    ppermute x15, starting transfers between devices, swap(): return lax.ppermute(values, 'pair', [(0, 1), (1, 0)])  30.1 us
    pallas_call x1, Pallas kernels, attend(): pl.pallas_call(attend_kernel, grid=(length // block,), in_specs=[pl.Block...  25.5 us
    dot_general x5, matrix products, contract_cols(): lax.dot_general(left_op, right_op, (((1,), (1,)), ((), ())), preferred_el...  23.8 us
  transfers between devices with their start and end apart: 70, of which 28 were waited for; matrix products, arithmetic and copies ran while one was open for 19% of the time, Pallas kernels for 10%

profile of v2, /device:TPU:0, one launch (start us, length us, event | category | flops | bytes accessed | tf_op | source)
XLA Modules:
  0.0 574.1 jit_solution(16769332800761053330)
XLA Ops:
  20.5 8.8 %collective-permute-done.12 = bf16[128,256]{1,0:T(8,128)(2,1)S(1)} collective-permute-done((bf16[128,256]{1,0:T(8,128)(2,1)S(1)}, bf16[128,256]{1,0:T(8,128)(2,1)S(1)}, u32[]{:S(2)}, u32[]{:S(2)}) %collective-permute-start.12) | collective-permute-done | bytes 65568 | tf_op jit(solution)/shard_map/ppermute | solution.py:243
  35.1 6.3 %collective-permute-done.23 = bf16[256,512]{0,1:T(8,128)(2,1)S(1)} collective-permute-done((bf16[256,512]{0,1:T(8,128)(2,1)S(1)}, bf16[256,512]{0,1:T(8,128)(2,1)S(1)}, u32[]{:S(2)}, u32[]{:S(2)}) %collective-permute-start.23) | collective-permute-done | bytes 262176 | tf_op jit(solution)/shard_map/ppermute | solution.py:243
  41.5 15.3 %collective-permute-done.22 = bf16[256,512]{0,1:T(8,128)(2,1)S(1)} collective-permute-done((bf16[256,512]{0,1:T(8,128)(2,1)S(1)}, bf16[256,512]{0,1:T(8,128)(2,1)S(1)}, u32[]{:S(2)}, u32[]{:S(2)}) %collective-permute-start.22) | collective-permute-done | bytes 262176 | tf_op jit(solution)/shard_map/ppermute | solution.py:243
  70.1 21.5 %collective-permute-start.24 = (bf16[128,512]{0,1:T(8,128)(2,1)}, bf16[128,512]{0,1:T(8,128)(2,1)S(1)}, u32[]{:S(2)}, u32[]{:S(2)}) collective-permute-start(bf16[128,512]{0,1:T(8,128)(2,1)} %get-tuple-element.156), channel_id=1, source_target_pairs={{0,4},{4,0},{1,5},{5,1},{2,6},{6,2},{3,7},{7,3},{8,12},{12,8},{9,1... | collective-permute-start | bytes 393224 | tf_op jit(solution)/shard_map/ppermute | solution.py:231
  99.3 6.1 %collective-permute-done.4 = bf16[512,1024]{1,0:T(8,128)(2,1)} collective-permute-done((bf16[512,1024]{1,0:T(8,128)(2,1)S(1)}, bf16[512,1024]{1,0:T(8,128)(2,1)}, u32[]{:S(2)}, u32[]{:S(2)}) %collective-permute-start.4) | collective-permute-done | bytes 1048608 | tf_op jit(solution)/shard_map/ppermute | solution.py:235
  109.1 13.1 %collective-permute-done.27 = bf16[256,512]{0,1:T(8,128)(2,1)S(1)} collective-permute-done((bf16[256,512]{0,1:T(8,128)(2,1)S(1)}, bf16[256,512]{0,1:T(8,128)(2,1)S(1)}, u32[]{:S(2)}, u32[]{:S(2)}) %collective-permute-start.27) | collective-permute-done | bytes 262176 | tf_op jit(solution)/shard_map/ppermute | solution.py:243
  123.7 13.2 %collective-permute-done.26 = bf16[256,512]{0,1:T(8,128)(2,1)S(1)} collective-permute-done((bf16[256,512]{0,1:T(8,128)(2,1)S(1)}, bf16[256,512]{0,1:T(8,128)(2,1)S(1)}, u32[]{:S(2)}, u32[]{:S(2)}) %collective-permute-start.26) | collective-permute-done | bytes 262176 | tf_op jit(solution)/shard_map/ppermute | solution.py:243
  165.0 25.5 %attend.1 = (bf16[2048,256]{1,0:T(8,128)(2,1)}, f32[4,2048]{1,0:T(4,128)}) custom-call(bf16[2048,768]{1,0:T(8,128)(2,1)} %copy.77.q_ref.k_ref.v_ref, bf16[2048,768]{1,0:T(8,128)(2,1)} %copy.77.q_ref.k_ref.v_ref, bf16[512,2048]{1,0:T(8,128)(2,1)} %slice_bitcast_fusion.vt_ref.kt_ref), custom_call_target="tpu_custom_call" | custom-call | tf_op jit(solution)/shard_map/attend/pallas_call | solution.py:99
  203.1 6.0 %collective-permute-done.15 = bf16[512,256]{1,0:T(8,128)(2,1)S(1)} collective-permute-done((bf16[512,256]{1,0:T(8,128)(2,1)S(1)}, bf16[512,256]{1,0:T(8,128)(2,1)S(1)}, u32[]{:S(2)}, u32[]{:S(2)}) %collective-permute-start.15) | collective-permute-done | bytes 262176 | tf_op jit(solution)/shard_map/ppermute | solution.py:235
  225.1 10.7 %fusion.30 = f32[1024,2048]{1,0:T(8,128)} fusion(bf16[1024,2048]{0,1:T(8,128)(2,1)} %all-gather.6.cloned.1.call-done, bf16[512,1024]{1,0:T(8,128)(2,1)} %collective-permute-done.19, bf16[512,1024]{1,0:T(8,128)(2,1)} %copy-done.25), kind=kOutput, calls=%fused_computation.76 | convolution fusion | flops 4299161600 | bytes 14680064 | tf_op jit(solution)/shard_map/dot_general | solution.py:482
  235.8 9.2 %fusion.48 = f32[1024,1024]{1,0:T(8,128)S(1)} fusion(bf16[1024,2048]{0,1:T(8,128)(2,1)} %all-gather.8.cloned.1.call-done, f32[1024,2048]{1,0:T(8,128)} %fusion.30), kind=kOutput, calls=%fused_computation.189 | convolution fusion | flops 4313841664 | bytes 16777216 | tf_op jit(solution)/shard_map/dot_general | solution.py:219
  256.5 12.8 %fusion.6 = bf16[1024,2048]{1,0:T(8,128)(2,1)S(1)} fusion(f32[1024,2048]{1,0:T(8,128)} %fusion.30, bf16[1024,2048]{0,1:T(8,128)(2,1)} %all-gather.8.cloned.1.call-done, bf16[512,1024]{1,0:T(8,128)(2,1)} %collective-permute-done.29, bf16[512,1024]{1,0:T(8,128)(2,1)} %get-tuple-element.105), kind=kOutput, calls=%fused_computation.8 | convolution fusion | flops 4341104640 | bytes 18874368 | tf_op jit(solution)/shard_map/dot_general | solution.py:494
  277.2 8.0 %convolution_convert_fusion.1 = bf16[1024,2048]{1,0:T(8,128)(2,1)} fusion(bf16[512,1024]{1,0:T(8,128)(2,1)} %collective-permute-done.29, bf16[512,1024]{1,0:T(8,128)(2,1)} %get-tuple-element.105, f32[1024,2048]{1,0:T(8,128)S(1)} %bitcast.92), kind=kOutput, calls=%fused_computation.12 | convolution fusion | flops 4320133120 | bytes 14680064 | tf_op jit(solution)/shard_map/dot_general | solution.py:213
  285.2 9.4 %convolution_convert_fusion = bf16[1024,2048]{1,0:T(8,128)(2,1)} fusion(bf16[1024,2048]{1,0:T(8,128)(2,1)} %copy-done.54, bf16[512,1024]{1,0:T(8,128)(2,1)} %collective-permute-done.19, bf16[512,1024]{1,0:T(8,128)(2,1)} %copy-done.25), kind=kOutput, calls=%fused_computation.11 | convolution fusion | flops 4301258752 | bytes 10485760 | tf_op jit(solution)/shard_map/dot_general | solution.py:213
  319.2 7.5 %collective-permute-done.33 = bf16[512,256]{1,0:T(8,128)(2,1)S(1)} collective-permute-done((bf16[512,256]{1,0:T(8,128)(2,1)S(1)}, bf16[512,256]{1,0:T(8,128)(2,1)S(1)}, u32[]{:S(2)}, u32[]{:S(2)}) %collective-permute-start.33) | collective-permute-done | bytes 262176 | tf_op jit(solution)/shard_map/ppermute | solution.py:235
  326.7 8.7 %collective-permute-done.32 = bf16[512,256]{1,0:T(8,128)(2,1)S(1)} collective-permute-done((bf16[512,256]{1,0:T(8,128)(2,1)S(1)}, bf16[512,256]{1,0:T(8,128)(2,1)S(1)}, u32[]{:S(2)}, u32[]{:S(2)}) %collective-permute-start.32) | collective-permute-done | bytes 262176 | tf_op jit(solution)/shard_map/ppermute | solution.py:235
  336.6 34.4 %attend_back.1 = bf16[2048,768]{1,0:T(8,128)(2,1)} custom-call(bf16[2048,768]{1,0:T(8,128)(2,1)} %copy.77.q_ref.k_ref.v_ref, bf16[2048,768]{1,0:T(8,128)(2,1)} %copy.77.q_ref.k_ref.v_ref, bf16[2048,768]{1,0:T(8,128)(2,1)} %copy.77.q_ref.k_ref.v_ref, bf16[512,2048]{1,0:T(8,128)(2,1)} %slice_bitcast_fusion.vt_ref.kt_ref, ...), custom_call_target="tpu_custom_call" | custom-call | tf_op jit(solution)/shard_map/attend_back/pallas_call | solution.py:189
  400.6 10.2 %collective-permute-done.39 = bf16[512,512]{1,0:T(8,128)(2,1)S(1)} collective-permute-done((bf16[512,512]{1,0:T(8,128)(2,1)S(1)}, bf16[512,512]{1,0:T(8,128)(2,1)S(1)}, u32[]{:S(2)}, u32[]{:S(2)}) %collective-permute-start.39) | collective-permute-done | bytes 524320 | tf_op jit(solution)/shard_map/ppermute | solution.py:235
  412.6 8.8 %collective-permute-done.42 = bf16[512,512]{1,0:T(8,128)(2,1)S(1)} collective-permute-done((bf16[512,512]{1,0:T(8,128)(2,1)S(1)}, bf16[512,512]{1,0:T(8,128)(2,1)S(1)}, u32[]{:S(2)}, u32[]{:S(2)}) %collective-permute-start.42) | collective-permute-done | bytes 524320 | tf_op jit(solution)/shard_map/ppermute | solution.py:235
  427.2 12.9 %collective-permute-done.43 = bf16[512,512]{1,0:T(8,128)(2,1)S(1)} collective-permute-done((bf16[512,512]{1,0:T(8,128)(2,1)}, bf16[512,512]{1,0:T(8,128)(2,1)S(1)}, u32[]{:S(2)}, u32[]{:S(2)}) %collective-permute-start.43) | collective-permute-done | bytes 524320 | tf_op jit(solution)/shard_map/ppermute | solution.py:235
  440.1 10.2 %collective-permute-done.37 = bf16[512,512]{1,0:T(8,128)(2,1)} collective-permute-done((bf16[512,512]{1,0:T(8,128)(2,1)}, bf16[512,512]{1,0:T(8,128)(2,1)}, u32[]{:S(2)}, u32[]{:S(2)}) %collective-permute-start.37) | collective-permute-done | bytes 524320 | tf_op jit(solution)/shard_map/ppermute | solution.py:235
  493.6 42.5 %reduce-scatter.6.cloned.1.call-done = bf16[256,2048]{1,0:T(8,128)(2,1)} async-done(((bf16[1024,2048]{1,0:T(8,128)(2,1)}), bf16[256,2048]{1,0:T(8,128)(2,1)}) %reduce-scatter.6.cloned.1.call-update) | async-done | bytes 1048592 | tf_op jit(solution)/shard_map/reduce_scatter | solution.py:513
  547.4 6.7 %collective-permute-done.53 = bf16[256,512]{1,0:T(8,128)(2,1)S(1)} collective-permute-done((bf16[256,512]{1,0:T(8,128)(2,1)S(1)}, bf16[256,512]{1,0:T(8,128)(2,1)S(1)}, u32[]{:S(2)}, u32[]{:S(2)}) %collective-permute-start.53) | collective-permute-done | bytes 262176 | tf_op jit(solution)/shard_map/ppermute | solution.py:243
  554.1 8.9 %collective-permute-done.52 = bf16[256,512]{1,0:T(8,128)(2,1)S(1)} collective-permute-done((bf16[256,512]{1,0:T(8,128)(2,1)S(1)}, bf16[256,512]{1,0:T(8,128)(2,1)S(1)}, u32[]{:S(2)}, u32[]{:S(2)}) %collective-permute-start.52) | collective-permute-done | bytes 262176 | tf_op jit(solution)/shard_map/ppermute | solution.py:243
  (364 shorter events, 241.2 us)
Async XLA Ops:
  7.2 140.9 %all-gather.4.cloned.1.call-start = ((), (), s32[]{:S(2)}) async-start(), calls=%async_computation.3 | async-start | bytes 3276800 | tf_op jit(solution)/shard_map/all_gather | solution.py:451
  30.3 194.8 %all-gather.6.cloned.1.call-start = ((), (), s32[]{:S(2)}) async-start(), calls=%async_computation.4 | async-start | bytes 5242880 | tf_op jit(solution)/shard_map/all_gather | solution.py:459
  33.3 23.5 %collective-permute-start.22 = (bf16[256,512]{0,1:T(8,128)(2,1)S(1)}, bf16[256,512]{0,1:T(8,128)(2,1)S(1)}, u32[]{:S(2)}, u32[]{:S(2)}) collective-permute-start(bf16[256,512]{0,1:T(8,128)(2,1)S(1)} %maximum_select_fusion.2), channel_id=1, source_target_pairs={{0,2},{1,3},{2,0},{3,1},{4,6},{5,7},{6,4},{7,5},{8,10},{9,11},{10,... | collective-permute-start | bytes 786440 | tf_op jit(solution)/shard_map/ppermute | solution.py:243
  33.4 23.4 %collective-permute-start.21 = (bf16[256,512]{0,1:T(8,128)(2,1)S(1)}, bf16[256,512]{0,1:T(8,128)(2,1)S(1)}, u32[]{:S(2)}, u32[]{:S(2)}) collective-permute-start(bf16[256,512]{0,1:T(8,128)(2,1)S(1)} %maximum_select_fusion.2), channel_id=1, source_target_pairs={{0,1},{1,2},{2,3},{3,0},{4,5},{5,6},{6,7},{7,4},{8,9},{9,10},{10,1... | collective-permute-start | bytes 786440 | tf_op jit(solution)/shard_map/ppermute | solution.py:243
  57.9 177.9 %all-gather.8.cloned.1.call-start = ((), (), s32[]{:S(2)}) async-start(), calls=%async_computation.5 | async-start | bytes 5242880 | tf_op jit(solution)/shard_map/all_gather | solution.py:466
  62.7 33.6 %collective-permute-start.1 = (bf16[512,1024]{1,0:T(8,128)(2,1)}, bf16[512,1024]{1,0:T(8,128)(2,1)}, u32[]{:S(2)}, u32[]{:S(2)}) collective-permute-start(bf16[512,1024]{1,0:T(8,128)(2,1)} %fusion.17), channel_id=1, source_target_pairs={{0,1},{1,0},{6,7},{7,6},{8,9},{9,8},{14,15},{15,14},{16,17},{17,16... | collective-permute-start | bytes 3145736 | tf_op jit(solution)/shard_map/ppermute | solution.py:235
  66.7 38.8 %collective-permute-start.4 = (bf16[512,1024]{1,0:T(8,128)(2,1)S(1)}, bf16[512,1024]{1,0:T(8,128)(2,1)}, u32[]{:S(2)}, u32[]{:S(2)}) collective-permute-start(bf16[512,1024]{1,0:T(8,128)(2,1)S(1)} %collective-permute-done.3), channel_id=1, source_target_pairs={{1,0},{6,7},{9,8},{14,15},{17,16},{22,23},{25,24},{30,31}} | collective-permute-start | bytes 3145736 | tf_op jit(solution)/shard_map/ppermute | solution.py:235
  68.1 54.2 %collective-permute-start.7 = (bf16[512,1024]{1,0:T(8,128)(2,1)S(1)}, bf16[512,1024]{1,0:T(8,128)(2,1)}, u32[]{:S(2)}, u32[]{:S(2)}) collective-permute-start(bf16[512,1024]{1,0:T(8,128)(2,1)S(1)} %collective-permute-done.6), channel_id=1, source_target_pairs={{1,0},{6,7},{9,8},{14,15},{17,16},{22,23},{25,24},{30,31}} | collective-permute-start | bytes 3145736 | tf_op jit(solution)/shard_map/ppermute | solution.py:235
  70.1 24.4 %collective-permute-start.24 = (bf16[128,512]{0,1:T(8,128)(2,1)}, bf16[128,512]{0,1:T(8,128)(2,1)S(1)}, u32[]{:S(2)}, u32[]{:S(2)}) collective-permute-start(bf16[128,512]{0,1:T(8,128)(2,1)} %get-tuple-element.156), channel_id=1, source_target_pairs={{0,4},{4,0},{1,5},{5,1},{2,6},{6,2},{3,7},{7,3},{8,12},{12,8},{9,1... | collective-permute-start | bytes 393224 | tf_op jit(solution)/shard_map/ppermute | solution.py:231
  91.6 50.8 %collective-permute-start = (bf16[512,1024]{1,0:T(8,128)(2,1)}, bf16[512,1024]{1,0:T(8,128)(2,1)}, u32[]{:S(2)}, u32[]{:S(2)}) collective-permute-start(bf16[512,1024]{1,0:T(8,128)(2,1)} %fusion.17), channel_id=1, source_target_pairs={{0,4},{1,5},{6,2},{7,3},{8,12},{9,13},{14,10},{15,11},{16,20},{17,... | collective-permute-start | bytes 3145736 | tf_op jit(solution)/shard_map/ppermute | solution.py:235
  96.2 26.0 %collective-permute-start.27 = (bf16[256,512]{0,1:T(8,128)(2,1)S(1)}, bf16[256,512]{0,1:T(8,128)(2,1)S(1)}, u32[]{:S(2)}, u32[]{:S(2)}) collective-permute-start(bf16[256,512]{0,1:T(8,128)(2,1)S(1)} %maximum_select_fusion.3), channel_id=1, source_target_pairs={{0,3},{1,0},{2,1},{3,2},{4,7},{5,4},{6,5},{7,6},{8,11},{9,8},{10,9... | collective-permute-start | bytes 786440 | tf_op jit(solution)/shard_map/ppermute | solution.py:243
  96.3 46.1 %collective-permute-start.2 = (bf16[512,1024]{1,0:T(8,128)(2,1)}, bf16[512,1024]{1,0:T(8,128)(2,1)}, u32[]{:S(2)}, u32[]{:S(2)}) collective-permute-start(bf16[512,1024]{1,0:T(8,128)(2,1)} %collective-permute-done.1), channel_id=1, source_target_pairs={{0,4},{1,5},{6,2},{7,3},{8,12},{9,13},{14,10},{15,11},{16,20},{17,... | collective-permute-start | bytes 3145736 | tf_op jit(solution)/shard_map/ppermute | solution.py:235
  106.8 35.6 %collective-permute-start.5 = (bf16[512,1024]{1,0:T(8,128)(2,1)S(1)}, bf16[512,1024]{1,0:T(8,128)(2,1)}, u32[]{:S(2)}, u32[]{:S(2)}) collective-permute-start(bf16[512,1024]{1,0:T(8,128)(2,1)S(1)} %broadcast_select_fusion.1), channel_id=1, source_target_pairs={{0,4},{1,5},{6,2},{7,3},{8,12},{9,13},{14,10},{15,11},{16,20},{17,... | collective-permute-start | bytes 3145736 | tf_op jit(solution)/shard_map/ppermute | solution.py:235
  142.1 298.0 %reduce-scatter.4.cloned.1.call-start = ((), (), s32[]{:S(2)}) async-start(), calls=%async_computation.6 | async-start | bytes 3276800 | tf_op jit(solution)/shard_map/reduce_scatter | solution.py:525
  150.6 61.2 %collective-permute-start.18 = (bf16[4,128,1024]{2,1,0:T(8,128)(2,1)}, bf16[4,128,1024]{2,1,0:T(8,128)(2,1)S(1)}, u32[]{:S(2)}, u32[]{:S(2)}) collective-permute-start(bf16[4,128,1024]{2,1,0:T(8,128)(2,1)} %pad_maximum_fusion.11), channel_id=1, source_target_pairs={{0,4},{4,0},{1,5},{5,1},{2,6},{6,2},{3,7},{7,3},{8,12},{12,8},{9,1... | collective-permute-start | bytes 3145736 | tf_op jit(solution)/shard_map/ppermute | solution.py:231
  317.8 63.3 %collective-permute-start.44 = (bf16[4,1,128,1024]{3,2,1,0:T(8,128)(2,1)}, bf16[4,1,128,1024]{3,2,1,0:T(8,128)(2,1)}, u32[]{:S(2)}, u32[]{:S(2)}) collective-permute-start(bf16[4,1,128,1024]{3,2,1,0:T(8,128)(2,1)} %constant_dynamic-slice_fusion.6), channel_id=1, source_target_pairs={{0,4},{4,0},{1,5},{5,1},{2,6},{6,2},{3,7},{7,3},{8,12},{12,8},{9,1... | collective-permute-start | bytes 3145736 | tf_op jit(solution)/shard_map/ppermute | solution.py:231
  386.6 97.7 %reduce-scatter.8.cloned.1.call-start = ((), (), s32[]{:S(2)}) async-start(), calls=%async_computation.8 | async-start | bytes 5242880 | tf_op jit(solution)/shard_map/reduce_scatter | solution.py:512
  387.2 148.9 %reduce-scatter.6.cloned.1.call-start = ((), (), s32[]{:S(2)}) async-start(), calls=%async_computation.7 | async-start | bytes 5242880 | tf_op jit(solution)/shard_map/reduce_scatter | solution.py:513
  400.0 40.1 %collective-permute-start.35 = (bf16[512,512]{1,0:T(8,128)(2,1)}, bf16[512,512]{1,0:T(8,128)(2,1)S(1)}, u32[]{:S(2)}, u32[]{:S(2)}) collective-permute-start(bf16[512,512]{1,0:T(8,128)(2,1)} %get-tuple-element.28), channel_id=1, source_target_pairs={{0,4},{4,0},{1,5},{5,1},{2,6},{6,2},{3,7},{7,3},{8,12},{12,8},{9,1... | collective-permute-start | bytes 1572872 | tf_op jit(solution)/shard_map/ppermute | solution.py:231
  400.2 23.6 %collective-permute-start.36 = (bf16[512,512]{1,0:T(8,128)(2,1)S(1)}, bf16[512,512]{1,0:T(8,128)(2,1)S(1)}, u32[]{:S(2)}, u32[]{:S(2)}) collective-permute-start(bf16[512,512]{1,0:T(8,128)(2,1)S(1)} %get-tuple-element.30), channel_id=1, source_target_pairs={{0,4},{4,0},{1,5},{5,1},{2,6},{6,2},{3,7},{7,3},{8,12},{12,8},{9,1... | collective-permute-start | bytes 1572872 | tf_op jit(solution)/shard_map/ppermute | solution.py:231
  424.7 25.7 %collective-permute-start.37 = (bf16[512,512]{1,0:T(8,128)(2,1)}, bf16[512,512]{1,0:T(8,128)(2,1)}, u32[]{:S(2)}, u32[]{:S(2)}) collective-permute-start(bf16[512,512]{1,0:T(8,128)(2,1)} %add_convert_fusion.5), channel_id=1, source_target_pairs={{0,1},{1,0},{2,3},{3,2},{4,5},{5,4},{6,7},{7,6},{8,9},{9,8},{10,11... | collective-permute-start | bytes 1572872 | tf_op jit(solution)/shard_map/ppermute | solution.py:235
  486.4 54.3 %collective-permute-start.55 = (bf16[256,512]{1,0:T(8,128)(2,1)}, bf16[256,512]{1,0:T(8,128)(2,1)S(1)}, u32[]{:S(2)}, u32[]{:S(2)}) collective-permute-start(bf16[256,512]{1,0:T(8,128)(2,1)} %get-tuple-element.119), channel_id=1, source_target_pairs={{0,3},{1,0},{2,1},{3,2},{4,7},{5,4},{6,5},{7,6},{8,11},{9,8},{10,9... | collective-permute-start | bytes 786440 | tf_op jit(solution)/shard_map/ppermute | solution.py:243
  488.9 52.9 %collective-permute-start.57 = (bf16[256,512]{1,0:T(8,128)(2,1)}, bf16[256,512]{1,0:T(8,128)(2,1)}, u32[]{:S(2)}, u32[]{:S(2)}) collective-permute-start(bf16[256,512]{1,0:T(8,128)(2,1)} %get-tuple-element.120), channel_id=1, source_target_pairs={{0,1},{1,2},{2,3},{3,0},{4,5},{5,6},{6,7},{7,4},{8,9},{9,10},{10,1... | collective-permute-start | bytes 786440 | tf_op jit(solution)/shard_map/ppermute | solution.py:243
  488.9 52.9 %collective-permute-start.56 = (bf16[256,512]{1,0:T(8,128)(2,1)}, bf16[256,512]{1,0:T(8,128)(2,1)}, u32[]{:S(2)}, u32[]{:S(2)}) collective-permute-start(bf16[256,512]{1,0:T(8,128)(2,1)} %get-tuple-element.121), channel_id=1, source_target_pairs={{0,2},{1,3},{2,0},{3,1},{4,6},{5,7},{6,4},{7,5},{8,10},{9,11},{10,... | collective-permute-start | bytes 786440 | tf_op jit(solution)/shard_map/ppermute | solution.py:243
  (105 other events, 955.5 us)
Sparse Core Ops, SparseCore 0:
  30.4 38.3 all-gather.3
  70.6 52.4 all-gather.5
  142.2 50.6 all-gather.7
  386.8 37.7 reduce-scatter.3
  427.4 53.2 reduce-scatter.7
  483.5 52.5 reduce-scatter.5

commit v3 on v2

--- a/solution.py
+++ b/solution.py
@@ -517,7 +517,7 @@
     w_own, w_other = halves(w_cols, 0)
     grad_a_other = contract_cols(grad_qkv, w_other).astype(bf16)
     grad_a_own = contract_cols(grad_qkv, w_own).astype(bf16)
-    grad_w = contract_rows(seq_a, after(grad_qkv, grad_a_own)).astype(bf16)
+    grad_w = contract_rows(seq_a, grad_qkv).astype(bf16)
     grad_a = sequence_sum(grad_a_own, grad_a_other)
     grad_o = grad_o.reshape(-1, 1, w_out.shape[1], attended.shape[1])
     grad_o = jnp.concatenate(jnp.split(grad_o, 2, axis=3), axis=1).reshape(model, -1)
@@ -525,13 +525,12 @@
     grad_w = lax.psum_scatter(grad_w, "outer", scatter_dimension=0, tiled=True)
     landed = grad_w
     grad_w, grad_o = grad_w[:, : 3 * width], grad_w[:, 3 * width :]
-    grad_o = collect(
-        [
-            grad_o[i * w_out.shape[1] : (i + 1) * w_out.shape[1], j * width : (j + 1) * width]
-            for i in range(2)
-            for j in range(2)
-        ]
-    ).T
+    grad_o = [
+        grad_o[i * w_out.shape[1] : (i + 1) * w_out.shape[1], j * width : (j + 1) * width]
+        for i in range(2)
+        for j in range(2)
+    ]
+    grad_o = collect(grad_o).T
     size = grad_w.shape[0] // 2
     parts = [
         send(

time: 580 us -> 579 us (level)
    dot_general x4, matrix products: 23.5 us -> 29.6 us  [contract_rows(): lax.dot_general(left_op, right_op, (((0,), (0,)), ((), ())), preferred_el...]
    unnamed x126 -> x108, local copies, waits for them, and re-layouts: 19.2 us -> 17.7 us
  transfers between devices with their start and end apart: 70 -> 70, of which waited for: 28 -> 29; matrix products, arithmetic and copies ran while one was open for 19% -> 19% of each run, Pallas kernels for 10% -> 10%
where the time goes in v3:
time: 579 us; the launch traced here: 574 us
  waiting for transfers between devices  211 us (36%)
  starting transfers between devices  113 us (20%)
  matrix products  78.2 us (14%)
  Pallas kernels  59.8 us (10%)
  other arithmetic  56.3 us (10%)
  local copies, waits for them, and re-layouts  40.8 us (7%)
  between operations  15.5 us (3%)
    ppermute x18, waiting for transfers between devices, shift(): lax.ppermute(values, 'head', [(i, (i + step) % HEADS) for i in range(HEAD...  77.6 us
    ppermute x26, waiting for transfers between devices, send(): lax.ppermute(values, LINE, [(a * HEADS + b, c * HEADS + d) for (a, b), (c...  75.4 us
    ppermute x26, starting transfers between devices, send(): lax.ppermute(values, LINE, [(a * HEADS + b, c * HEADS + d) for (a, b), (c...  56.5 us
    reduce_scatter x1, waiting for transfers between devices, layer(): lax.psum_scatter(grad_up, 'outer', scatter_dimension=0, tiled=True)  42.5 us
    pallas_call x1, Pallas kernels, attend_back(): pl.pallas_call(attend_back_kernel, grid=(length // block,), in_specs=[pl....  34.4 us
    ppermute x15, starting transfers between devices, swap(): return lax.ppermute(values, 'pair', [(0, 1), (1, 0)])  30.7 us
    dot_general x4, matrix products, contract_rows(): lax.dot_general(left_op, right_op, (((0,), (0,)), ((), ())), preferred_el...  29.6 us
    pallas_call x1, Pallas kernels, attend(): pl.pallas_call(attend_kernel, grid=(length // block,), in_specs=[pl.Block...  25.5 us
  transfers between devices with their start and end apart: 70, of which 29 were waited for; matrix products, arithmetic and copies ran while one was open for 19% of the time, Pallas kernels for 10%

profile of v3, /device:TPU:0, one launch (start us, length us, event | category | flops | bytes accessed | tf_op | source)
XLA Modules:
  0.0 573.8 jit_solution(6752490022308303159)
XLA Ops:
  20.5 8.8 %collective-permute-done.12 = bf16[128,256]{1,0:T(8,128)(2,1)S(1)} collective-permute-done((bf16[128,256]{1,0:T(8,128)(2,1)S(1)}, bf16[128,256]{1,0:T(8,128)(2,1)S(1)}, u32[]{:S(2)}, u32[]{:S(2)}) %collective-permute-start.12) | collective-permute-done | bytes 65568 | tf_op jit(solution)/shard_map/ppermute | solution.py:243
  35.1 6.3 %collective-permute-done.23 = bf16[256,512]{0,1:T(8,128)(2,1)S(1)} collective-permute-done((bf16[256,512]{0,1:T(8,128)(2,1)S(1)}, bf16[256,512]{0,1:T(8,128)(2,1)S(1)}, u32[]{:S(2)}, u32[]{:S(2)}) %collective-permute-start.23) | collective-permute-done | bytes 262176 | tf_op jit(solution)/shard_map/ppermute | solution.py:243
  41.4 15.3 %collective-permute-done.22 = bf16[256,512]{0,1:T(8,128)(2,1)S(1)} collective-permute-done((bf16[256,512]{0,1:T(8,128)(2,1)S(1)}, bf16[256,512]{0,1:T(8,128)(2,1)S(1)}, u32[]{:S(2)}, u32[]{:S(2)}) %collective-permute-start.22) | collective-permute-done | bytes 262176 | tf_op jit(solution)/shard_map/ppermute | solution.py:243
  70.0 21.6 %collective-permute-start.24 = (bf16[128,512]{0,1:T(8,128)(2,1)}, bf16[128,512]{0,1:T(8,128)(2,1)S(1)}, u32[]{:S(2)}, u32[]{:S(2)}) collective-permute-start(bf16[128,512]{0,1:T(8,128)(2,1)} %get-tuple-element.154), channel_id=1, source_target_pairs={{0,4},{4,0},{1,5},{5,1},{2,6},{6,2},{3,7},{7,3},{8,12},{12,8},{9,1... | collective-permute-start | bytes 393224 | tf_op jit(solution)/shard_map/ppermute | solution.py:231
  99.5 6.0 %collective-permute-done.4 = bf16[512,1024]{1,0:T(8,128)(2,1)} collective-permute-done((bf16[512,1024]{1,0:T(8,128)(2,1)S(1)}, bf16[512,1024]{1,0:T(8,128)(2,1)}, u32[]{:S(2)}, u32[]{:S(2)}) %collective-permute-start.4) | collective-permute-done | bytes 1048608 | tf_op jit(solution)/shard_map/ppermute | solution.py:235
  109.1 13.1 %collective-permute-done.27 = bf16[256,512]{0,1:T(8,128)(2,1)S(1)} collective-permute-done((bf16[256,512]{0,1:T(8,128)(2,1)S(1)}, bf16[256,512]{0,1:T(8,128)(2,1)S(1)}, u32[]{:S(2)}, u32[]{:S(2)}) %collective-permute-start.27) | collective-permute-done | bytes 262176 | tf_op jit(solution)/shard_map/ppermute | solution.py:243
  123.7 13.2 %collective-permute-done.26 = bf16[256,512]{0,1:T(8,128)(2,1)S(1)} collective-permute-done((bf16[256,512]{0,1:T(8,128)(2,1)S(1)}, bf16[256,512]{0,1:T(8,128)(2,1)S(1)}, u32[]{:S(2)}, u32[]{:S(2)}) %collective-permute-start.26) | collective-permute-done | bytes 262176 | tf_op jit(solution)/shard_map/ppermute | solution.py:243
  164.9 25.5 %attend.1 = (bf16[2048,256]{1,0:T(8,128)(2,1)}, f32[4,2048]{1,0:T(4,128)}) custom-call(bf16[2048,768]{1,0:T(8,128)(2,1)} %copy.77.q_ref.k_ref.v_ref, bf16[2048,768]{1,0:T(8,128)(2,1)} %copy.77.q_ref.k_ref.v_ref, bf16[512,2048]{1,0:T(8,128)(2,1)} %slice_bitcast_fusion.vt_ref.kt_ref), custom_call_target="tpu_custom_call" | custom-call | tf_op jit(solution)/shard_map/attend/pallas_call | solution.py:99
  225.1 10.7 %fusion.30 = f32[1024,2048]{1,0:T(8,128)} fusion(bf16[1024,2048]{0,1:T(8,128)(2,1)} %all-gather.6.cloned.1.call-done, bf16[512,1024]{1,0:T(8,128)(2,1)} %collective-permute-done.19, bf16[512,1024]{1,0:T(8,128)(2,1)} %copy-done.19), kind=kOutput, calls=%fused_computation.76 | convolution fusion | flops 4299161600 | bytes 14680064 | tf_op jit(solution)/shard_map/dot_general | solution.py:482
  235.8 9.0 %fusion.48 = f32[1024,1024]{1,0:T(8,128)S(1)} fusion(bf16[1024,2048]{0,1:T(8,128)(2,1)} %all-gather.8.cloned.1.call-done, f32[1024,2048]{1,0:T(8,128)} %fusion.30), kind=kOutput, calls=%fused_computation.189 | convolution fusion | flops 4313841664 | bytes 16777216 | tf_op jit(solution)/shard_map/dot_general | solution.py:219
  256.0 12.9 %fusion.6 = bf16[1024,2048]{1,0:T(8,128)(2,1)S(1)} fusion(f32[1024,2048]{1,0:T(8,128)} %fusion.30, bf16[1024,2048]{0,1:T(8,128)(2,1)} %all-gather.8.cloned.1.call-done, bf16[512,1024]{1,0:T(8,128)(2,1)} %collective-permute-done.29, bf16[512,1024]{1,0:T(8,128)(2,1)} %get-tuple-element.103), kind=kOutput, calls=%fused_computation.8 | convolution fusion | flops 4341104640 | bytes 18874368 | tf_op jit(solution)/shard_map/dot_general | solution.py:494
  276.9 10.9 %convolution_convert_fusion.1 = bf16[1024,2048]{1,0:T(8,128)(2,1)} fusion(bf16[512,1024]{1,0:T(8,128)(2,1)} %collective-permute-done.29, bf16[512,1024]{1,0:T(8,128)(2,1)} %get-tuple-element.103, f32[1024,2048]{1,0:T(8,128)} %fusion.30), kind=kOutput, calls=%fused_computation.12 | convolution fusion | flops 4320133120 | bytes 14680064 | tf_op jit(solution)/shard_map/dot_general | solution.py:213
  287.7 9.6 %convolution_convert_fusion = bf16[1024,2048]{1,0:T(8,128)(2,1)} fusion(bf16[1024,2048]{1,0:T(8,128)(2,1)} %copy-done.47, bf16[512,1024]{1,0:T(8,128)(2,1)} %collective-permute-done.19, bf16[512,1024]{1,0:T(8,128)(2,1)} %copy-done.19), kind=kOutput, calls=%fused_computation.11 | convolution fusion | flops 4301258752 | bytes 10485760 | tf_op jit(solution)/shard_map/dot_general | solution.py:213
  321.8 7.5 %collective-permute-done.33 = bf16[512,256]{1,0:T(8,128)(2,1)S(1)} collective-permute-done((bf16[512,256]{1,0:T(8,128)(2,1)S(1)}, bf16[512,256]{1,0:T(8,128)(2,1)S(1)}, u32[]{:S(2)}, u32[]{:S(2)}) %collective-permute-start.33) | collective-permute-done | bytes 262176 | tf_op jit(solution)/shard_map/ppermute | solution.py:235
  329.2 8.5 %collective-permute-done.32 = bf16[512,256]{1,0:T(8,128)(2,1)S(1)} collective-permute-done((bf16[512,256]{1,0:T(8,128)(2,1)S(1)}, bf16[512,256]{1,0:T(8,128)(2,1)S(1)}, u32[]{:S(2)}, u32[]{:S(2)}) %collective-permute-start.32) | collective-permute-done | bytes 262176 | tf_op jit(solution)/shard_map/ppermute | solution.py:235
  338.9 34.4 %attend_back.1 = bf16[2048,768]{1,0:T(8,128)(2,1)} custom-call(bf16[2048,768]{1,0:T(8,128)(2,1)} %copy.77.q_ref.k_ref.v_ref, bf16[2048,768]{1,0:T(8,128)(2,1)} %copy.77.q_ref.k_ref.v_ref, bf16[2048,768]{1,0:T(8,128)(2,1)} %copy.77.q_ref.k_ref.v_ref, bf16[512,2048]{1,0:T(8,128)(2,1)} %slice_bitcast_fusion.vt_ref.kt_ref, ...), custom_call_target="tpu_custom_call" | custom-call | tf_op jit(solution)/shard_map/attend_back/pallas_call | solution.py:189
  373.2 7.8 %convolution_convert_fusion.6 = bf16[1024,768]{0,1:T(8,128)(2,1)} fusion(bf16[2048,768]{1,0:T(8,128)(2,1)} %attend_back.1, bf16[512,1024]{1,0:T(8,128)(2,1)} %get-tuple-element.116, bf16[512,1024]{1,0:T(8,128)(2,1)} %get-tuple-element.100, bf16[512,1024]{1,0:T(8,128)(2,1)} %get-tuple-element.99, bf16[512,1024]{1,0:T(8,128)(2,1)} %get-tuple-element.96), kind=kOutput, calls=%fused_computation.73 | convolution fusion | flops 3238789120 | bytes 8912896 | tf_op jit(solution)/shard_map/dot_general | solution.py:213
  400.5 10.2 %collective-permute-done.39 = bf16[512,512]{1,0:T(8,128)(2,1)S(1)} collective-permute-done((bf16[512,512]{1,0:T(8,128)(2,1)S(1)}, bf16[512,512]{1,0:T(8,128)(2,1)S(1)}, u32[]{:S(2)}, u32[]{:S(2)}) %collective-permute-start.39) | collective-permute-done | bytes 524320 | tf_op jit(solution)/shard_map/ppermute | solution.py:235
  412.4 9.0 %collective-permute-done.42 = bf16[512,512]{1,0:T(8,128)(2,1)S(1)} collective-permute-done((bf16[512,512]{1,0:T(8,128)(2,1)S(1)}, bf16[512,512]{1,0:T(8,128)(2,1)S(1)}, u32[]{:S(2)}, u32[]{:S(2)}) %collective-permute-start.42) | collective-permute-done | bytes 524320 | tf_op jit(solution)/shard_map/ppermute | solution.py:235
  427.2 12.7 %collective-permute-done.43 = bf16[512,512]{1,0:T(8,128)(2,1)S(1)} collective-permute-done((bf16[512,512]{1,0:T(8,128)(2,1)}, bf16[512,512]{1,0:T(8,128)(2,1)S(1)}, u32[]{:S(2)}, u32[]{:S(2)}) %collective-permute-start.43) | collective-permute-done | bytes 524320 | tf_op jit(solution)/shard_map/ppermute | solution.py:235
  439.9 10.4 %collective-permute-done.37 = bf16[512,512]{1,0:T(8,128)(2,1)} collective-permute-done((bf16[512,512]{1,0:T(8,128)(2,1)}, bf16[512,512]{1,0:T(8,128)(2,1)}, u32[]{:S(2)}, u32[]{:S(2)}) %collective-permute-start.37) | collective-permute-done | bytes 524320 | tf_op jit(solution)/shard_map/ppermute | solution.py:235
  493.6 42.5 %reduce-scatter.6.cloned.1.call-done = bf16[256,2048]{1,0:T(8,128)(2,1)} async-done(((bf16[1024,2048]{1,0:T(8,128)(2,1)}), bf16[256,2048]{1,0:T(8,128)(2,1)}) %reduce-scatter.6.cloned.1.call-update) | async-done | bytes 1048592 | tf_op jit(solution)/shard_map/reduce_scatter | solution.py:513
  547.3 6.7 %collective-permute-done.53 = bf16[256,512]{1,0:T(8,128)(2,1)S(1)} collective-permute-done((bf16[256,512]{1,0:T(8,128)(2,1)S(1)}, bf16[256,512]{1,0:T(8,128)(2,1)S(1)}, u32[]{:S(2)}, u32[]{:S(2)}) %collective-permute-start.53) | collective-permute-done | bytes 262176 | tf_op jit(solution)/shard_map/ppermute | solution.py:243
  554.0 8.9 %collective-permute-done.52 = bf16[256,512]{1,0:T(8,128)(2,1)S(1)} collective-permute-done((bf16[256,512]{1,0:T(8,128)(2,1)S(1)}, bf16[256,512]{1,0:T(8,128)(2,1)S(1)}, u32[]{:S(2)}, u32[]{:S(2)}) %collective-permute-start.52) | collective-permute-done | bytes 262176 | tf_op jit(solution)/shard_map/ppermute | solution.py:243
  (345 shorter events, 236.8 us)
Async XLA Ops:
  7.2 140.8 %all-gather.4.cloned.1.call-start = ((), (), s32[]{:S(2)}) async-start(), calls=%async_computation.3 | async-start | bytes 3276800 | tf_op jit(solution)/shard_map/all_gather | solution.py:451
  30.2 194.8 %all-gather.6.cloned.1.call-start = ((), (), s32[]{:S(2)}) async-start(), calls=%async_computation.4 | async-start | bytes 5242880 | tf_op jit(solution)/shard_map/all_gather | solution.py:459
  33.3 23.5 %collective-permute-start.22 = (bf16[256,512]{0,1:T(8,128)(2,1)S(1)}, bf16[256,512]{0,1:T(8,128)(2,1)S(1)}, u32[]{:S(2)}, u32[]{:S(2)}) collective-permute-start(bf16[256,512]{0,1:T(8,128)(2,1)S(1)} %maximum_select_fusion.2), channel_id=1, source_target_pairs={{0,2},{1,3},{2,0},{3,1},{4,6},{5,7},{6,4},{7,5},{8,10},{9,11},{10,... | collective-permute-start | bytes 786440 | tf_op jit(solution)/shard_map/ppermute | solution.py:243
  33.4 23.4 %collective-permute-start.21 = (bf16[256,512]{0,1:T(8,128)(2,1)S(1)}, bf16[256,512]{0,1:T(8,128)(2,1)S(1)}, u32[]{:S(2)}, u32[]{:S(2)}) collective-permute-start(bf16[256,512]{0,1:T(8,128)(2,1)S(1)} %maximum_select_fusion.2), channel_id=1, source_target_pairs={{0,1},{1,2},{2,3},{3,0},{4,5},{5,6},{6,7},{7,4},{8,9},{9,10},{10,1... | collective-permute-start | bytes 786440 | tf_op jit(solution)/shard_map/ppermute | solution.py:243
  57.9 177.9 %all-gather.8.cloned.1.call-start = ((), (), s32[]{:S(2)}) async-start(), calls=%async_computation.5 | async-start | bytes 5242880 | tf_op jit(solution)/shard_map/all_gather | solution.py:466
  62.7 33.7 %collective-permute-start.1 = (bf16[512,1024]{1,0:T(8,128)(2,1)}, bf16[512,1024]{1,0:T(8,128)(2,1)}, u32[]{:S(2)}, u32[]{:S(2)}) collective-permute-start(bf16[512,1024]{1,0:T(8,128)(2,1)} %fusion.17), channel_id=1, source_target_pairs={{0,1},{1,0},{6,7},{7,6},{8,9},{9,8},{14,15},{15,14},{16,17},{17,16... | collective-permute-start | bytes 3145736 | tf_op jit(solution)/shard_map/ppermute | solution.py:235
  66.7 38.8 %collective-permute-start.4 = (bf16[512,1024]{1,0:T(8,128)(2,1)S(1)}, bf16[512,1024]{1,0:T(8,128)(2,1)}, u32[]{:S(2)}, u32[]{:S(2)}) collective-permute-start(bf16[512,1024]{1,0:T(8,128)(2,1)S(1)} %collective-permute-done.3), channel_id=1, source_target_pairs={{1,0},{6,7},{9,8},{14,15},{17,16},{22,23},{25,24},{30,31}} | collective-permute-start | bytes 3145736 | tf_op jit(solution)/shard_map/ppermute | solution.py:235
  68.0 54.2 %collective-permute-start.7 = (bf16[512,1024]{1,0:T(8,128)(2,1)S(1)}, bf16[512,1024]{1,0:T(8,128)(2,1)}, u32[]{:S(2)}, u32[]{:S(2)}) collective-permute-start(bf16[512,1024]{1,0:T(8,128)(2,1)S(1)} %collective-permute-done.6), channel_id=1, source_target_pairs={{1,0},{6,7},{9,8},{14,15},{17,16},{22,23},{25,24},{30,31}} | collective-permute-start | bytes 3145736 | tf_op jit(solution)/shard_map/ppermute | solution.py:235
  70.0 24.5 %collective-permute-start.24 = (bf16[128,512]{0,1:T(8,128)(2,1)}, bf16[128,512]{0,1:T(8,128)(2,1)S(1)}, u32[]{:S(2)}, u32[]{:S(2)}) collective-permute-start(bf16[128,512]{0,1:T(8,128)(2,1)} %get-tuple-element.154), channel_id=1, source_target_pairs={{0,4},{4,0},{1,5},{5,1},{2,6},{6,2},{3,7},{7,3},{8,12},{12,8},{9,1... | collective-permute-start | bytes 393224 | tf_op jit(solution)/shard_map/ppermute | solution.py:231
  91.7 50.7 %collective-permute-start = (bf16[512,1024]{1,0:T(8,128)(2,1)}, bf16[512,1024]{1,0:T(8,128)(2,1)}, u32[]{:S(2)}, u32[]{:S(2)}) collective-permute-start(bf16[512,1024]{1,0:T(8,128)(2,1)} %fusion.17), channel_id=1, source_target_pairs={{0,4},{1,5},{6,2},{7,3},{8,12},{9,13},{14,10},{15,11},{16,20},{17,... | collective-permute-start | bytes 3145736 | tf_op jit(solution)/shard_map/ppermute | solution.py:235
  96.3 25.9 %collective-permute-start.27 = (bf16[256,512]{0,1:T(8,128)(2,1)S(1)}, bf16[256,512]{0,1:T(8,128)(2,1)S(1)}, u32[]{:S(2)}, u32[]{:S(2)}) collective-permute-start(bf16[256,512]{0,1:T(8,128)(2,1)S(1)} %maximum_select_fusion.3), channel_id=1, source_target_pairs={{0,3},{1,0},{2,1},{3,2},{4,7},{5,4},{6,5},{7,6},{8,11},{9,8},{10,9... | collective-permute-start | bytes 786440 | tf_op jit(solution)/shard_map/ppermute | solution.py:243
  96.3 46.0 %collective-permute-start.2 = (bf16[512,1024]{1,0:T(8,128)(2,1)}, bf16[512,1024]{1,0:T(8,128)(2,1)}, u32[]{:S(2)}, u32[]{:S(2)}) collective-permute-start(bf16[512,1024]{1,0:T(8,128)(2,1)} %collective-permute-done.1), channel_id=1, source_target_pairs={{0,4},{1,5},{6,2},{7,3},{8,12},{9,13},{14,10},{15,11},{16,20},{17,... | collective-permute-start | bytes 3145736 | tf_op jit(solution)/shard_map/ppermute | solution.py:235
  106.8 35.6 %collective-permute-start.5 = (bf16[512,1024]{1,0:T(8,128)(2,1)S(1)}, bf16[512,1024]{1,0:T(8,128)(2,1)}, u32[]{:S(2)}, u32[]{:S(2)}) collective-permute-start(bf16[512,1024]{1,0:T(8,128)(2,1)S(1)} %broadcast_select_fusion.1), channel_id=1, source_target_pairs={{0,4},{1,5},{6,2},{7,3},{8,12},{9,13},{14,10},{15,11},{16,20},{17,... | collective-permute-start | bytes 3145736 | tf_op jit(solution)/shard_map/ppermute | solution.py:235
  142.0 297.8 %reduce-scatter.4.cloned.1.call-start = ((), (), s32[]{:S(2)}) async-start(), calls=%async_computation.6 | async-start | bytes 3276800 | tf_op jit(solution)/shard_map/reduce_scatter | solution.py:525
  150.5 61.3 %collective-permute-start.18 = (bf16[4,128,1024]{2,1,0:T(8,128)(2,1)}, bf16[4,128,1024]{2,1,0:T(8,128)(2,1)S(1)}, u32[]{:S(2)}, u32[]{:S(2)}) collective-permute-start(bf16[4,128,1024]{2,1,0:T(8,128)(2,1)} %pad_maximum_fusion.11), channel_id=1, source_target_pairs={{0,4},{4,0},{1,5},{5,1},{2,6},{6,2},{3,7},{7,3},{8,12},{12,8},{9,1... | collective-permute-start | bytes 3145736 | tf_op jit(solution)/shard_map/ppermute | solution.py:231
  320.2 60.9 %collective-permute-start.44 = (bf16[4,1,128,1024]{3,2,1,0:T(8,128)(2,1)}, bf16[4,1,128,1024]{3,2,1,0:T(8,128)(2,1)}, u32[]{:S(2)}, u32[]{:S(2)}) collective-permute-start(bf16[4,1,128,1024]{3,2,1,0:T(8,128)(2,1)} %constant_dynamic-slice_fusion.6), channel_id=1, source_target_pairs={{0,4},{4,0},{1,5},{5,1},{2,6},{6,2},{3,7},{7,3},{8,12},{12,8},{9,1... | collective-permute-start | bytes 3145736 | tf_op jit(solution)/shard_map/ppermute | solution.py:231
  386.5 97.7 %reduce-scatter.8.cloned.1.call-start = ((), (), s32[]{:S(2)}) async-start(), calls=%async_computation.8 | async-start | bytes 5242880 | tf_op jit(solution)/shard_map/reduce_scatter | solution.py:512
  387.1 149.0 %reduce-scatter.6.cloned.1.call-start = ((), (), s32[]{:S(2)}) async-start(), calls=%async_computation.7 | async-start | bytes 5242880 | tf_op jit(solution)/shard_map/reduce_scatter | solution.py:513
  399.9 40.0 %collective-permute-start.35 = (bf16[512,512]{1,0:T(8,128)(2,1)}, bf16[512,512]{1,0:T(8,128)(2,1)S(1)}, u32[]{:S(2)}, u32[]{:S(2)}) collective-permute-start(bf16[512,512]{1,0:T(8,128)(2,1)} %get-tuple-element.27), channel_id=1, source_target_pairs={{0,4},{4,0},{1,5},{5,1},{2,6},{6,2},{3,7},{7,3},{8,12},{12,8},{9,1... | collective-permute-start | bytes 1572872 | tf_op jit(solution)/shard_map/ppermute | solution.py:231
  400.1 23.6 %collective-permute-start.36 = (bf16[512,512]{1,0:T(8,128)(2,1)S(1)}, bf16[512,512]{1,0:T(8,128)(2,1)S(1)}, u32[]{:S(2)}, u32[]{:S(2)}) collective-permute-start(bf16[512,512]{1,0:T(8,128)(2,1)S(1)} %get-tuple-element.29), channel_id=1, source_target_pairs={{0,4},{4,0},{1,5},{5,1},{2,6},{6,2},{3,7},{7,3},{8,12},{12,8},{9,1... | collective-permute-start | bytes 1572872 | tf_op jit(solution)/shard_map/ppermute | solution.py:231
  424.6 25.7 %collective-permute-start.37 = (bf16[512,512]{1,0:T(8,128)(2,1)}, bf16[512,512]{1,0:T(8,128)(2,1)}, u32[]{:S(2)}, u32[]{:S(2)}) collective-permute-start(bf16[512,512]{1,0:T(8,128)(2,1)} %add_convert_fusion.5), channel_id=1, source_target_pairs={{0,1},{1,0},{2,3},{3,2},{4,5},{5,4},{6,7},{7,6},{8,9},{9,8},{10,11... | collective-permute-start | bytes 1572872 | tf_op jit(solution)/shard_map/ppermute | solution.py:235
  486.3 54.3 %collective-permute-start.55 = (bf16[256,512]{1,0:T(8,128)(2,1)}, bf16[256,512]{1,0:T(8,128)(2,1)S(1)}, u32[]{:S(2)}, u32[]{:S(2)}) collective-permute-start(bf16[256,512]{1,0:T(8,128)(2,1)} %get-tuple-element.117), channel_id=1, source_target_pairs={{0,3},{1,0},{2,1},{3,2},{4,7},{5,4},{6,5},{7,6},{8,11},{9,8},{10,9... | collective-permute-start | bytes 786440 | tf_op jit(solution)/shard_map/ppermute | solution.py:243
  488.8 52.9 %collective-permute-start.57 = (bf16[256,512]{1,0:T(8,128)(2,1)}, bf16[256,512]{1,0:T(8,128)(2,1)}, u32[]{:S(2)}, u32[]{:S(2)}) collective-permute-start(bf16[256,512]{1,0:T(8,128)(2,1)} %get-tuple-element.118), channel_id=1, source_target_pairs={{0,1},{1,2},{2,3},{3,0},{4,5},{5,6},{6,7},{7,4},{8,9},{9,10},{10,1... | collective-permute-start | bytes 786440 | tf_op jit(solution)/shard_map/ppermute | solution.py:243
  488.8 52.9 %collective-permute-start.56 = (bf16[256,512]{1,0:T(8,128)(2,1)}, bf16[256,512]{1,0:T(8,128)(2,1)}, u32[]{:S(2)}, u32[]{:S(2)}) collective-permute-start(bf16[256,512]{1,0:T(8,128)(2,1)} %get-tuple-element.119), channel_id=1, source_target_pairs={{0,2},{1,3},{2,0},{3,1},{4,6},{5,7},{6,4},{7,5},{8,10},{9,11},{10,... | collective-permute-start | bytes 786440 | tf_op jit(solution)/shard_map/ppermute | solution.py:243
  (96 other events, 851.0 us)
Sparse Core Ops, SparseCore 0:
  30.3 38.3 all-gather.3
  70.6 52.4 all-gather.5
  142.2 50.6 all-gather.7
  386.6 37.7 reduce-scatter.3
  427.2 53.3 reduce-scatter.7
  483.4 52.5 reduce-scatter.5
